TPU v7x, 32 devices: a whole 2x2x4 slice. The times are simulated.
32 devices in a mesh: col: 4 (over z), row: 8 (over y, x, core).
Axes of the slice: x: 2, y: 2, z: 4, core: 2. Of those that a mesh axis runs over, the one named last changes fastest.
Arguments:
- mask: int32 [4096, 65536], P('row', 'col')
- user_emb: bfloat16 [4096, 64], P(('row', 'col'))
- item_emb: bfloat16 [65536, 64], P(('col', 'row'))
- queries: int32 [256], replicated
Outputs:
- output 1: bfloat16 [4096, 64], P(('row', 'col'))
- output 2: bfloat16 [65536, 64], P(('col', 'row'))
- output 3: float32 [256, 65536], P(None, ('col', 'row'))
All inputs are finite; a program needn't handle non-finite values.
Results may differ from a plain program's by a relative error of at most 0.00673458.
Values are sent between devices in bfloat16 or wider.
A program may use at most 1 GiB of HBM per device.

v0:
```python
import jax
import jax.numpy as jnp
from jax import lax
from jax.sharding import PartitionSpec as P

LAYERS = 3


def norm_block(mask_blk):
    deg_user = lax.psum(jnp.sum(mask_blk, axis=1), 'col')
    deg_item = lax.psum(jnp.sum(mask_blk, axis=0), 'row')
    inv_user = lax.rsqrt(jnp.maximum(deg_user, 1).astype(jnp.float32))
    inv_item = lax.rsqrt(jnp.maximum(deg_item, 1).astype(jnp.float32))
    return (inv_user[:, None] * mask_blk.astype(jnp.float32) * inv_item[None, :]).astype(jnp.bfloat16)


def query_scores(final_user, final_item, queries, shard_pos):
    rows_local = final_user.shape[0]
    local_idx = queries - shard_pos * rows_local
    owned = (local_idx >= 0) & (local_idx < rows_local)
    picked = jnp.take(final_user, jnp.clip(local_idx, 0, rows_local - 1), axis=0)
    picked = jnp.where(owned[:, None], picked, jnp.zeros_like(picked))
    picked = lax.psum(picked, ('row', 'col'))
    return lax.dot_general(picked, final_item, (((1,), (1,)), ((), ())), preferred_element_type=jnp.float32)


def solution(mesh):
    n_col = mesh.shape['col']
    contract_rows = (((0,), (0,)), ((), ()))

    def device_step(mask_blk, user_shard, item_shard, queries):
        norm_adj = norm_block(mask_blk)
        user_cur = user_shard
        item_cur = item_shard
        user_sum = user_shard.astype(jnp.float32)
        item_sum = item_shard.astype(jnp.float32)
        for layer_idx in range(LAYERS):
            item_panel = lax.all_gather(item_cur, 'row', axis=0, tiled=True)
            user_part = jnp.dot(norm_adj, item_panel, preferred_element_type=jnp.float32)
            user_next = lax.psum_scatter(user_part, 'col', scatter_dimension=0, tiled=True).astype(jnp.bfloat16)
            user_panel = lax.all_gather(user_cur, 'col', axis=0, tiled=True)
            item_part = lax.dot_general(norm_adj, user_panel, contract_rows, preferred_element_type=jnp.float32)
            item_next = lax.psum_scatter(item_part, 'row', scatter_dimension=0, tiled=True).astype(jnp.bfloat16)
            user_sum = user_sum + user_next.astype(jnp.float32)
            item_sum = item_sum + item_next.astype(jnp.float32)
            user_cur = user_next
            item_cur = item_next
        final_user = (user_sum / (LAYERS + 1)).astype(jnp.bfloat16)
        final_item = (item_sum / (LAYERS + 1)).astype(jnp.bfloat16)
        shard_pos = lax.axis_index('row') * n_col + lax.axis_index('col')
        scores = query_scores(final_user, final_item, queries, shard_pos)
        return final_user, final_item, scores

    return jax.shard_map(device_step, mesh=mesh, in_specs=(P('row', 'col'), P(('row', 'col'), None), P(('col', 'row'), None), P()), out_specs=(P(('row', 'col'), None), P(('col', 'row'), None), P(None, ('col', 'row'))), check_vma=False)
```

profile of v0, /device:TPU:0, one launch (start us, length us, event | category | flops | bytes accessed | tf_op | source)
XLA Modules:
  0.0 458.8 jit_solution(3118370437419042439)
XLA Ops:
  7.2 0.0 all-reduce.2.cloned.1.call-start
  7.2 13.1 %fusion = (s32[512]{0:T(512)S(1)}, s32[16384]{0:T(1024)}) fusion(s32[512,16384]{1,0:T(8,128)} %param.4), kind=kLoop, calls=%fused_computation.11 | loop fusion | flops 16760320 | bytes 33622016 | tf_op jit(solution)/shard_map/reduce_sum | solution.py:10
  20.3 0.0 all-reduce.2.cloned.1.call-update
  20.4 0.0 all-gather.4.cloned.1.call-start
  20.4 0.7 all-gather.4.cloned.1.call-update
  21.1 0.0 reduce-scatter.9.cloned.1.call-start
  21.2 10.0 %psum.21 = s32[512]{0:T(512)S(1)} all-reduce(s32[512]{0:T(512)S(1)} %get-tuple-element.3), channel_id=1, replica_groups=mesh['col'=4,'row'=8] {'col'}, use_global_device_ids=true, to_apply=%region_1.0 | all-reduce | flops 512 | bytes 4096 | tf_op jit(solution)/shard_map/psum | solution.py:10
  31.2 13.2 %all_gather.19 = bf16[512,64]{0,1:T(8,128)(2,1)S(1)} all-gather(bf16[128,64]{0,1:T(8,128)(2,1)S(1)} %copy-done.6), channel_id=1, replica_groups=mesh['col'=4,'row'=8] {'col'}, dimensions={0}, use_global_device_ids=true | all-gather | bytes 81920 | tf_op jit(solution)/shard_map/all_gather | solution.py:41
  44.4 31.9 %all-reduce.2.cloned.1.call-done = s32[16384]{0:T(1024)} async-done(((s32[16384]{0:T(1024)}), s32[16384]{0:T(1024)}) %all-reduce.2.cloned.1.call-update) | async-done | bytes 65552 | tf_op jit(solution)/shard_map/psum | solution.py:11
  76.3 0.9 convert_rsqrt_fusion
  77.2 13.1 %multiply_convert_fusion = bf16[512,16384]{1,0:T(8,128)(2,1)S(1)} fusion(s32[512,16384]{1,0:T(8,128)} %param.4, f32[16384]{0:T(1024)S(1)} %convert_rsqrt_fusion, f32[512]{0:T(512)S(1)} %convert_rsqrt_fusion.1), kind=kLoop, calls=%fused_computation.1 | loop fusion | flops 33554432 | bytes 50399232 | tf_op jit(solution)/shard_map/convert_element_type | solution.py:14
  90.3 5.7 %copy-done = bf16[512,16384]{1,0:T(8,128)(2,1)} copy-done((bf16[512,16384]{1,0:T(8,128)(2,1)}, bf16[512,16384]{1,0:T(8,128)(2,1)S(1)}, u32[]{:S(2)}) %copy-start) | copy-done | bytes 16777240
  96.0 5.0 %fusion.5 = f32[16384,64]{0,1:T(8,128)} fusion(bf16[512,64]{0,1:T(8,128)(2,1)S(1)} %all_gather.19, bf16[512,16384]{1,0:T(8,128)(2,1)S(1)} %multiply_convert_fusion), kind=kOutput, calls=%fused_computation.16 | convolution fusion | flops 1073741824 | bytes 21037056 | tf_op jit(solution)/shard_map/dot_general | solution.py:42
  101.0 0.0 reduce-scatter.7.cloned.1.call-start
  101.1 4.1 all-gather.4.cloned.1.call-done
  105.1 12.2 %fusion.1 = f32[512,64]{0,1:T(8,128)} fusion(bf16[512,16384]{1,0:T(8,128)(2,1)} %copy-done, bf16[16384,64]{0,1:T(8,128)(2,1)} %all-gather.4.cloned.1.call-done), kind=kOutput, calls=%fused_computation.12 | convolution fusion | flops 1073741824 | bytes 19005440 | tf_op jit(solution)/shard_map/dot_general | solution.py:39
  117.4 0.0 reduce-scatter.7.cloned.1.call-update
  117.4 0.0 all-gather.6.cloned.1.call-start
  117.4 41.9 %reduce-scatter.9.cloned.1.call-done = f32[2048,64]{0,1:T(8,128)} async-done(((f32[16384,64]{0,1:T(8,128)}), f32[2048,64]{0,1:T(8,128)}) %reduce-scatter.9.cloned.1.call-update) | async-done | bytes 524304 | tf_op jit(solution)/shard_map/reduce_scatter | solution.py:43
  159.3 1.8 convert_element_type.67
  161.1 0.0 all-gather.6.cloned.1.call-update
  161.1 0.0 reduce-scatter.11.cloned.1.call-start
  161.2 20.3 %reduce-scatter.7.cloned.1.call-done = f32[128,64]{0,1:T(8,128)} async-done(((f32[512,64]{0,1:T(8,128)}), f32[128,64]{0,1:T(8,128)}) %reduce-scatter.7.cloned.1.call-update) | async-done | bytes 32784 | tf_op jit(solution)/shard_map/reduce_scatter | solution.py:40
  181.4 0.8 convert_element_type.65
  182.2 13.4 %all_gather.21 = bf16[512,64]{0,1:T(8,128)(2,1)S(1)} all-gather(bf16[128,64]{0,1:T(8,128)(2,1)S(1)} %convert_element_type.65), channel_id=1, replica_groups=mesh['col'=4,'row'=8] {'col'}, dimensions={0}, use_global_device_ids=true | all-gather | bytes 81920 | tf_op jit(solution)/shard_map/all_gather | solution.py:41
  195.6 13.8 %all-gather.6.cloned.1.call-done = bf16[16384,64]{0,1:T(8,128)(2,1)} async-done(((bf16[2048,64]{0,1:T(8,128)(2,1)}), bf16[16384,64]{0,1:T(8,128)(2,1)}) %all-gather.6.cloned.1.call-update) | async-done | bytes 2097168 | tf_op jit(solution)/shard_map/all_gather | solution.py:38
  209.4 12.2 %fusion.2 = f32[512,64]{0,1:T(8,128)} fusion(bf16[512,16384]{1,0:T(8,128)(2,1)} %copy-done, bf16[16384,64]{0,1:T(8,128)(2,1)} %all-gather.6.cloned.1.call-done), kind=kOutput, calls=%fused_computation.13 | convolution fusion | flops 1073741824 | bytes 19005440 | tf_op jit(solution)/shard_map/dot_general | solution.py:39
  221.7 0.0 reduce-scatter.13.cloned.1.call-start
  221.7 10.7 %fusion.6 = f32[16384,64]{0,1:T(8,128)} fusion(bf16[512,64]{0,1:T(8,128)(2,1)S(1)} %all_gather.21, bf16[512,16384]{1,0:T(8,128)(2,1)} %copy-done), kind=kOutput, calls=%fused_computation.17 | convolution fusion | flops 1073741824 | bytes 21037056 | tf_op jit(solution)/shard_map/dot_general | solution.py:42
  232.5 0.0 reduce-scatter.17.cloned.1.call-start
  232.5 8.7 %reduce-scatter.11.cloned.1.call-done = f32[128,64]{0,1:T(8,128)} async-done(((f32[512,64]{0,1:T(8,128)}), f32[128,64]{0,1:T(8,128)}) %reduce-scatter.11.cloned.1.call-update) | async-done | bytes 32784 | tf_op jit(solution)/shard_map/reduce_scatter | solution.py:40
  241.3 0.8 convert_element_type.68
  242.0 13.2 %all_gather.23 = bf16[512,64]{0,1:T(8,128)(2,1)S(1)} all-gather(bf16[128,64]{0,1:T(8,128)(2,1)S(1)} %convert_element_type.68), channel_id=1, replica_groups=mesh['col'=4,'row'=8] {'col'}, dimensions={0}, use_global_device_ids=true | all-gather | bytes 81920 | tf_op jit(solution)/shard_map/all_gather | solution.py:41
  255.2 10.8 %fusion.7 = f32[16384,64]{0,1:T(8,128)} fusion(bf16[512,64]{0,1:T(8,128)(2,1)S(1)} %all_gather.23, bf16[512,16384]{1,0:T(8,128)(2,1)} %copy-done), kind=kOutput, calls=%fused_computation.18 | convolution fusion | flops 1073741824 | bytes 21037056 | tf_op jit(solution)/shard_map/dot_general | solution.py:42
  266.0 0.0 all-gather.8.cloned.1.call-start
  266.1 27.5 %reduce-scatter.13.cloned.1.call-done = f32[2048,64]{0,1:T(8,128)} async-done(((f32[16384,64]{0,1:T(8,128)}), f32[2048,64]{0,1:T(8,128)}) %reduce-scatter.13.cloned.1.call-update) | async-done | bytes 524304 | tf_op jit(solution)/shard_map/reduce_scatter | solution.py:43
  293.6 54.2 %reduce-scatter.17.cloned.1.call-done = f32[2048,64]{0,1:T(8,128)} async-done(((f32[16384,64]{0,1:T(8,128)}), f32[2048,64]{0,1:T(8,128)}) %reduce-scatter.17.cloned.1.call-update) | async-done | bytes 524304 | tf_op jit(solution)/shard_map/reduce_scatter | solution.py:43
  347.7 2.0 multiply_convert_fusion.1
  349.8 0.3 reduce-scatter.15.cloned.1.call-start
  350.1 27.7 %all-gather.8.cloned.1.call-done = bf16[16384,64]{0,1:T(8,128)(2,1)} async-done(((bf16[2048,64]{0,1:T(8,128)(2,1)}), bf16[16384,64]{0,1:T(8,128)(2,1)}) %all-gather.8.cloned.1.call-update) | async-done | bytes 2097168 | tf_op jit(solution)/shard_map/all_gather | solution.py:38
  377.8 12.2 %fusion.3 = f32[512,64]{0,1:T(8,128)} fusion(bf16[512,16384]{1,0:T(8,128)(2,1)} %copy-done, bf16[16384,64]{0,1:T(8,128)(2,1)} %all-gather.8.cloned.1.call-done), kind=kOutput, calls=%fused_computation.14 | convolution fusion | flops 1073741824 | bytes 19005440 | tf_op jit(solution)/shard_map/dot_general | solution.py:39
  390.1 19.5 %reduce-scatter.15.cloned.1.call-done = f32[128,64]{0,1:T(8,128)} async-done(((f32[512,64]{0,1:T(8,128)}), f32[128,64]{0,1:T(8,128)}) %reduce-scatter.15.cloned.1.call-update) | async-done | bytes 32784 | tf_op jit(solution)/shard_map/reduce_scatter | solution.py:40
  409.6 0.8 multiply_convert_fusion.2
  410.3 0.1 copy.7
  410.5 0.9 gather_fusion
  411.3 0.1 select_select_fusion
  411.5 38.7 %psum.23 = bf16[256,64]{1,0:T(8,128)(2,1)S(1)} all-reduce(bf16[256,64]{1,0:T(8,128)(2,1)S(1)} %select_select_fusion), channel_id=1, replica_groups=mesh['col'=4,'row'=8] {'row','col'}, use_global_device_ids=true, to_apply=%region_10.11 | all-reduce | flops 16384 | bytes 65536 | tf_op jit(solution)/shard_map/psum | solution.py:23
  450.2 1.7 fusion.4
  (26 shorter events, 0.2 us)
Async XLA Ops:
  7.2 24.0 %copy-start.6 = (bf16[128,64]{0,1:T(8,128)(2,1)S(1)}, bf16[128,64]{0,1:T(8,128)(2,1)}, u32[]{:S(2)}) copy-start(bf16[128,64]{0,1:T(8,128)(2,1)} %param.5) | copy-start | bytes 49156
  7.2 69.1 %all-reduce.2.cloned.1.call-start = ((), (), s32[]{:S(2)}) async-start(), calls=%async_computation.6 | async-start | bytes 131072 | tf_op jit(solution)/shard_map/psum | solution.py:11
  20.4 84.8 %all-gather.4.cloned.1.call-start = ((), (), s32[]{:S(2)}) async-start(), calls=%async_computation.7 | async-start | bytes 2359296 | tf_op jit(solution)/shard_map/all_gather | solution.py:38
  21.1 138.2 %reduce-scatter.9.cloned.1.call-start = ((), (), s32[]{:S(2)}) async-start(), calls=%async_computation.9 | async-start | bytes 4718592 | tf_op jit(solution)/shard_map/reduce_scatter | solution.py:43
  90.3 5.7 %copy-start = (bf16[512,16384]{1,0:T(8,128)(2,1)}, bf16[512,16384]{1,0:T(8,128)(2,1)S(1)}, u32[]{:S(2)}) copy-start(bf16[512,16384]{1,0:T(8,128)(2,1)S(1)} %multiply_convert_fusion) | copy-start | bytes 50331652
  101.0 80.4 %reduce-scatter.7.cloned.1.call-start = ((), (), s32[]{:S(2)}) async-start(), calls=%async_computation.8 | async-start | bytes 163840 | tf_op jit(solution)/shard_map/reduce_scatter | solution.py:40
  117.4 92.1 %all-gather.6.cloned.1.call-start = ((), (), s32[]{:S(2)}) async-start(), calls=%async_computation.10 | async-start | bytes 2359296 | tf_op jit(solution)/shard_map/all_gather | solution.py:38
  161.1 80.1 %reduce-scatter.11.cloned.1.call-start = ((), (), s32[]{:S(2)}) async-start(), calls=%async_computation.11 | async-start | bytes 163840 | tf_op jit(solution)/shard_map/reduce_scatter | solution.py:40
  221.7 71.9 %reduce-scatter.13.cloned.1.call-start = ((), (), s32[]{:S(2)}) async-start(), calls=%async_computation.12 | async-start | bytes 4718592 | tf_op jit(solution)/shard_map/reduce_scatter | solution.py:43
  232.5 115.3 %copy-start.1 = (f32[2048,64]{0,1:T(8,128)S(1)}, f32[2048,64]{0,1:T(8,128)}, u32[]{:S(2)}) copy-start(f32[2048,64]{0,1:T(8,128)} %reduce-scatter.9.cloned.1.call-done) | copy-start | bytes 1572868
  232.5 115.3 %copy-start.3 = (bf16[2048,64]{0,1:T(8,128)(2,1)S(1)}, bf16[2048,64]{0,1:T(8,128)(2,1)}, u32[]{:S(2)}) copy-start(bf16[2048,64]{0,1:T(8,128)(2,1)} %param.6) | copy-start | bytes 786436
  232.5 115.2 %reduce-scatter.17.cloned.1.call-start = ((), (), s32[]{:S(2)}) async-start(), calls=%async_computation.15 | async-start | bytes 4718592 | tf_op jit(solution)/shard_map/reduce_scatter | solution.py:43
  266.0 124.0 %copy-start.8 = (s32[256]{0:T(256)S(1)}, s32[256]{0:T(256)}, u32[]{:S(2)}) copy-start(s32[256]{0:T(256)} %param.7) | copy-start | bytes 3076
  266.0 143.6 %copy-start.4 = (f32[128,64]{0,1:T(8,128)S(1)}, f32[128,64]{0,1:T(8,128)}, u32[]{:S(2)}) copy-start(f32[128,64]{0,1:T(8,128)} %reduce-scatter.7.cloned.1.call-done) | copy-start | bytes 98308
  266.0 143.6 %copy-start.5 = (f32[128,64]{0,1:T(8,128)S(1)}, f32[128,64]{0,1:T(8,128)}, u32[]{:S(2)}) copy-start(f32[128,64]{0,1:T(8,128)} %reduce-scatter.11.cloned.1.call-done) | copy-start | bytes 98308
  266.0 111.8 %all-gather.8.cloned.1.call-start = ((), (), s32[]{:S(2)}) async-start(), calls=%async_computation.13 | async-start | bytes 2359296 | tf_op jit(solution)/shard_map/all_gather | solution.py:38
  349.8 102.2 %copy-start.2 = (bf16[2048,64]{0,1:T(8,128)(2,1)}, bf16[2048,64]{0,1:T(8,128)(2,1)S(1)}, u32[]{:S(2)}) copy-start(bf16[2048,64]{0,1:T(8,128)(2,1)S(1)} %get-tuple-element.7) | copy-start | bytes 786436
  349.8 59.8 %reduce-scatter.15.cloned.1.call-start = ((), (), s32[]{:S(2)}) async-start(), calls=%async_computation.14 | async-start | bytes 163840 | tf_op jit(solution)/shard_map/reduce_scatter | solution.py:40
  410.3 41.6 %copy-start.7 = (bf16[128,64]{0,1:T(8,128)(2,1)}, bf16[128,64]{0,1:T(8,128)(2,1)S(1)}, u32[]{:S(2)}) copy-start(bf16[128,64]{0,1:T(8,128)(2,1)S(1)} %multiply_convert_fusion.2) | copy-start | bytes 49156
Sparse Core Ops, SparseCore 0:
  20.5 55.7 all-reduce.1
  78.2 26.8 all-gather.3
  108.5 50.7 reduce-scatter.8
  162.0 19.3 reduce-scatter.6
  183.8 25.6 all-gather.5
  221.8 19.3 reduce-scatter.10
  244.6 48.9 reduce-scatter.12
  296.9 50.7 reduce-scatter.16
  350.2 27.5 all-gather.7
  390.1 19.3 reduce-scatter.14
where the time goes:
time: 460 us; the launch traced here: 459 us
  waiting for transfers between devices  250 us (54%)
  blocking collectives  88.6 us (19%)
  matrix products  64.8 us (14%)
  other arithmetic  33.4 us (7%)
  between operations  14.3 us (3%)
  local copies, waits for them, and re-layouts  6.74 us (1%)
    reduce_scatter x3, waiting for transfers between devices, device_step(): lax.psum_scatter(item_part, 'row', scatter_dimension=0, tiled=True)  124 us
    reduce_scatter x3, waiting for transfers between devices, device_step(): lax.psum_scatter(user_part, 'col', scatter_dimension=0, tiled=True)  48.5 us
    all_gather x3, waiting for transfers between devices, device_step(): item_panel = lax.all_gather(item_cur, 'row', axis=0, tiled=True)  45.6 us
    all_gather x3, blocking collectives, device_step(): user_panel = lax.all_gather(user_cur, 'col', axis=0, tiled=True)  39.8 us
    psum x1, blocking collectives, query_scores(): picked = lax.psum(picked, ('row', 'col'))  38.7 us
    dot_general x3, matrix products, device_step(): jnp.dot(norm_adj, item_panel, preferred_element_type=jnp.float32)  36.6 us
    psum x1, waiting for transfers between devices, norm_block(): deg_item = lax.psum(jnp.sum(mask_blk, axis=0), 'row')  31.9 us
    dot_general x3, matrix products, device_step(): lax.dot_general(norm_adj, user_panel, contract_rows, preferred_element_ty...  26.5 us
  transfers between devices with their start and end apart: 10, of which 10 were waited for; matrix products, arithmetic and copies ran while one was open for 12% of the time, Pallas kernels for 0%

commit v1 on v0

v1 whole, which is shorter than its diff:
```python
import jax
import jax.numpy as jnp
from jax import lax
from jax.experimental import pallas as pl
from jax.experimental.pallas import tpu as pltpu
from jax.sharding import PartitionSpec as P

LAYERS = 3
EMB = 64
HALF = EMB // 2
NT = (((1,), (1,)), ((), ()))
NN = (((1,), (0,)), ((), ()))
TN = (((0,), (0,)), ((), ()))
F32 = jnp.float32
BF16 = jnp.bfloat16
STAGES = 4
N_COPIES = 112


def dot(lhs, rhs, dims):
    return lax.dot_general(lhs, rhs, dims, preferred_element_type=F32)


def kernel(mask_ref, item_ref, user_ref, query_ref, fu_ref, fi_ref, pick_ref,
           adj, stage, panel, upan, psend, drecv, sacc, hop1, rown, isum, usum,
           colacc, rowacc, deg_send, deg_recv, deg_own, deg_in, deg_fin, deg_oth,
           udeg, udeg_in, invu, upart, uin, pk, stage_sem, send_sem, recv_sem):
    c = lax.axis_index('col')
    r = lax.axis_index('row')
    users = rowacc.shape[0]
    width = adj.shape[2]
    rows = stage.shape[1]
    per_slot = users // rows
    core, cx, cy = r % 2, (r // 2) % 2, r // 4

    def plane(d, k):
        return ((cy + d // 2) % 2) * 4 + ((cx + d % 2) % 2) * 2 + (core + k) % 2

    def zpeer(k):
        return ((c // 2 + k // 2) % 2) * 2 + (c % 2 + k % 2) % 2

    slots = {d * 2 + k: (c, plane(d, k)) for d in range(4) for k in range(2)}
    partner, xn, yn, dg = slots[1], slots[2], slots[4], slots[6]
    zn = [None] + [(zpeer(k), r) for k in (1, 2, 3)]

    started = []

    def send(src, dst, device):
        n = len(started)
        copy = pltpu.make_async_remote_copy(
            src_ref=src, dst_ref=dst, send_sem=send_sem.at[n], recv_sem=recv_sem.at[n],
            device_id=device, device_id_type=pl.DeviceIdType.MESH)
        copy.start()
        started.append(copy)
        return copy

    def mask_copy(step):
        slot = step // per_slot
        part = step % per_slot
        col = plane(slot // 2, slot % 2) * width
        return pltpu.make_async_copy(
            mask_ref.at[pl.ds(pl.multiple_of(part * rows, rows), rows),
                        pl.ds(pl.multiple_of(col, width), width)],
            stage.at[step % STAGES], stage_sem.at[step % STAGES])

    steps = 8 * per_slot
    for s in range(STAGES):
        mask_copy(jnp.int32(s)).start()

    barrier = pltpu.get_barrier_semaphore()
    peers = (partner, xn, yn, dg, zn[1], zn[2], zn[3])
    for device in peers:
        pl.semaphore_signal(barrier, inc=1, device_id=device, device_id_type=pl.DeviceIdType.MESH)

    eye = (lax.broadcasted_iota(jnp.int32, (EMB, EMB), 0)
           == lax.broadcasted_iota(jnp.int32, (EMB, EMB), 1)).astype(BF16)
    items_t = dot(eye, item_ref[...], NT)
    users_t = dot(eye, user_ref[...], NT)
    isum[...] = items_t
    usum[...] = users_t
    panel[0, 0] = items_t.astype(BF16)
    upan[0, c] = users_t.astype(BF16)
    rowacc[...] = jnp.zeros_like(rowacc)
    colacc[...] = jnp.zeros_like(colacc)
    pl.semaphore_wait(barrier, len(peers))

    def gather_start(n):
        own = panel.at[n, 0]
        lo, hi = pl.ds(0, HALF), pl.ds(HALF, HALF)
        g = {}
        g['xa'] = send(own.at[lo], panel.at[n, 2, lo], xn)
        g['yb'] = send(own.at[hi], panel.at[n, 4, hi], yn)
        g['xb'] = send(own.at[hi], panel.at[n, 2, hi], xn)
        g['ya'] = send(own.at[lo], panel.at[n, 4, lo], yn)
        g['p0'] = send(own, panel.at[n, 1], partner)
        return g

    def gather_forward(n, g):
        lo, hi = pl.ds(0, HALF), pl.ds(HALF, HALF)
        g['xa'].wait_recv()
        g['da'] = send(panel.at[n, 2, lo], panel.at[n, 6, lo], yn)
        g['yb'].wait_recv()
        g['db'] = send(panel.at[n, 4, hi], panel.at[n, 6, hi], xn)
        g['xb'].wait_recv()
        g['p1'] = send(panel.at[n, 2], panel.at[n, 3], partner)
        g['ya'].wait_recv()
        g['p2'] = send(panel.at[n, 4], panel.at[n, 5], partner)

    def gather_last(n, g):
        g['da'].wait_recv()
        g['db'].wait_recv()
        g['p3'] = send(panel.at[n, 6], panel.at[n, 7], partner)

    def zgather_start(n):
        return [send(upan.at[n, c], upan.at[n, c], zn[k]) for k in (1, 2, 3)]

    def zgather_wait(n, g):
        for copy in g:
            copy.wait_recv()
        return jnp.concatenate([upan[n, k] for k in range(4)], axis=1)

    def zsum_start(n, acc):
        acc_t = acc.T
        for k in range(4):
            upart[n, k] = acc_t[:, k * 128:(k + 1) * 128]
        return [send(upart.at[n, zpeer(k)], uin.at[n, k - 1], zn[k]) for k in (1, 2, 3)]

    def zsum_wait(n, g):
        for copy in g:
            copy.wait_recv()
        total = (upart[n, c] + uin[n, 0]) + (uin[n, 1] + uin[n, 2])
        nxt = total.astype(BF16)
        usum[...] = usum[...] + nxt.astype(F32)
        return nxt

    gather0 = gather_start(0)
    zgather0 = zgather_start(0)

    def mask_step(step, carry):
        mask_copy(step).wait()
        slot = step // per_slot
        part = step % per_slot
        buf = step % STAGES

        def group(i, col):
            at = pl.multiple_of(i * 16, 16)
            x = stage[buf, pl.ds(at, 16), :].astype(F32)
            row = pl.multiple_of(part * rows + i * 16, 16)
            adj[slot, pl.ds(row, 16), :] = x.astype(BF16)
            lanes = x[:, :128]
            for t in range(1, width // 128):
                lanes = lanes + x[:, t * 128:(t + 1) * 128]
            rowacc[pl.ds(row, 16), :] += lanes
            return col + (x[:8] + x[8:])

        colacc[slot] += lax.fori_loop(0, rows // 16, group, jnp.zeros((8, width), F32), unroll=2)

        @pl.when(step + STAGES < steps)
        def _():
            mask_copy(step + STAGES).start()

        return carry

    lax.fori_loop(0, steps * 5 // 8, mask_step, 0)
    gather_forward(0, gather0)
    lax.fori_loop(steps * 5 // 8, steps, mask_step, 0)

    for d in range(4):
        deg_send[d:d + 1, :] = jnp.sum(colacc[2 * d + 1], axis=0, keepdims=True)
    dp = send(deg_send, deg_recv, partner)
    udeg[...] = dot(jnp.ones((8, 128), BF16), rowacc[...].astype(BF16), NT)
    zd = [send(udeg, udeg_in.at[k - 1], zn[k]) for k in (1, 2, 3)]
    mine = jnp.concatenate(
        [jnp.sum(colacc[2 * d], axis=0, keepdims=True) for d in range(4)], axis=0)
    dp.wait_recv()
    deg_own[...] = mine + deg_recv[...]
    ds = [send(deg_own, deg_in.at[0], xn), send(deg_own, deg_in.at[1], yn),
          send(deg_own, deg_in.at[2], dg)]
    gather_last(0, gather0)
    for copy in zd:
        copy.wait_recv()
    du = (udeg[...] + udeg_in[0]) + (udeg_in[1] + udeg_in[2])
    inv = lax.rsqrt(jnp.maximum(du, 1.0))
    invu[...] = jnp.broadcast_to(inv[0:1, :], (128, users)).T
    for copy in ds:
        copy.wait_recv()
    for d in range(4):
        total = ((deg_own[d:d + 1, :] + deg_in[0, (d ^ 1):(d ^ 1) + 1, :])
                 + (deg_in[1, (d ^ 2):(d ^ 2) + 1, :] + deg_in[2, (d ^ 3):(d ^ 3) + 1, :]))
        deg_fin[d:d + 1, :] = lax.rsqrt(jnp.maximum(total, 1.0))
    df = send(deg_fin, deg_oth, partner)

    def normalize(slot):
        d = slot // 2
        inv_item = (deg_oth if slot % 2 else deg_fin)[d:d + 1, :]

        def group(i, carry):
            at = pl.multiple_of(i * 16, 16)
            scale = (invu[pl.ds(at, 16), 0:1] * inv_item).astype(BF16)
            adj[slot, pl.ds(at, 16), :] = adj[slot, pl.ds(at, 16), :] * scale
            return carry

        lax.fori_loop(0, users // 16, group, 0, unroll=2)

    def items_start(n, u, first=False, between=None):
        p = {}
        for d in (3, 1, 2, 0):
            if first:
                normalize(2 * d + 1)
            psend[n, d] = dot(u, adj[2 * d + 1], NN)
            p[d] = send(psend.at[n, d], drecv.at[n, d], partner)
        s = {}
        for d in (3, 1, 2, 0):
            if first:
                normalize(2 * d)
            part = dot(u, adj[2 * d], NN)
            p[d].wait_recv()
            sacc[n, d] = part + drecv[n, d]
            lo, hi = pl.ds(0, HALF), pl.ds(HALF, HALF)
            if d == 3:
                s['x1'] = send(sacc.at[n, 3, lo], hop1.at[n, 0], xn)
                s['y1'] = send(sacc.at[n, 3, hi], hop1.at[n, 1], yn)
                if between is not None:
                    between()
            elif d == 1:
                s['xa'] = send(sacc.at[n, 1, lo], rown.at[n, 0], xn)
            elif d == 2:
                s['yb'] = send(sacc.at[n, 2, hi], rown.at[n, 3], yn)
        return s

    def items_mid(n, s):
        lo, hi = pl.ds(0, HALF), pl.ds(HALF, HALF)
        s['x1'].wait_recv()
        sacc[n, 2, lo] = sacc[n, 2, lo] + hop1[n, 0]
        s['ya'] = send(sacc.at[n, 2, lo], rown.at[n, 2], yn)
        s['y1'].wait_recv()
        sacc[n, 1, hi] = sacc[n, 1, hi] + hop1[n, 1]
        s['xb'] = send(sacc.at[n, 1, hi], rown.at[n, 1], xn)

    def items_finish(n, s):
        for key in ('xa', 'yb', 'ya', 'xb'):
            s[key].wait_recv()
        for h, at in ((0, pl.ds(0, HALF)), (1, pl.ds(HALF, HALF))):
            total = (sacc[n, 0, at] + rown[n, h]) + rown[n, 2 + h]
            nxt = total.astype(BF16)
            isum[at] = isum[at] + nxt.astype(F32)
            if n + 1 < LAYERS:
                panel[n + 1, 0, at] = nxt

    def user_partial(n, g):
        g['p0'].wait_recv()
        g['p1'].wait_recv()
        g['p2'].wait_recv()

        def one(j, acc):
            return acc + dot(adj[j], panel[n, j], NT)

        acc = lax.fori_loop(0, 7, one, jnp.zeros((users, EMB), F32))
        g['p3'].wait_recv()
        return acc + dot(adj[7], panel[n, 7], NT)

    u0 = zgather_wait(0, zgather0)
    df.wait_recv()
    s0 = items_start(0, u0, first=True)
    z0 = zsum_start(0, user_partial(0, gather0))
    items_mid(0, s0)
    upan[1, c] = zsum_wait(0, z0)
    zg1 = zgather_start(1)
    u1 = zgather_wait(1, zg1)
    items_finish(0, s0)
    g1 = gather_start(1)
    s1 = items_start(1, u1, between=lambda: gather_forward(1, g1))
    gather_last(1, g1)
    z1 = zsum_start(1, user_partial(1, g1))
    items_mid(1, s1)
    upan[2, c] = zsum_wait(1, z1)
    zg2 = zgather_start(2)
    u2 = zgather_wait(2, zg2)
    items_finish(1, s1)
    g2 = gather_start(2)
    s2 = items_start(2, u2, between=lambda: gather_forward(2, g2))
    gather_last(2, g2)
    z2 = zsum_start(2, user_partial(2, g2))
    items_mid(2, s2)
    zsum_wait(2, z2)
    final_user = (usum[...] / (LAYERS + 1)).astype(BF16)
    fu_ref[...] = final_user
    upan[3, c] = final_user
    zg3 = zgather_start(3)
    ufin = zgather_wait(3, zg3)
    local = query_ref[...] - r * users
    chosen = (lax.broadcasted_iota(jnp.int32, (users, local.shape[1]), 0)
              == jnp.broadcast_to(local, (users, local.shape[1]))).astype(F32).astype(BF16)
    pk[0] = dot(ufin, chosen, NN).astype(BF16)
    q = send(pk.at[0], pk.at[1], partner)
    q.wait_recv()
    pk[2] = pk[0] + pk[1]
    qs = [send(pk.at[2], pk.at[3], xn), send(pk.at[2], pk.at[4], yn), send(pk.at[2], pk.at[5], dg)]
    items_finish(2, s2)
    fi_ref[...] = (isum[...] / (LAYERS + 1)).astype(BF16)
    for copy in qs:
        copy.wait_recv()
    pick_ref[...] = (pk[2] + pk[3]) + (pk[4] + pk[5])
    for copy in started:
        copy.wait_send()


def propagate(mask_blk, user_shard, item_shard, queries):
    users, items = mask_blk.shape
    width = items // 8
    per = user_shard.shape[0]
    n_query = queries.shape[0]
    vmem = pl.BlockSpec(memory_space=pltpu.VMEM)
    scratch = [
        pltpu.VMEM((8, users, width), BF16),
        pltpu.VMEM((STAGES, users // 2, width), jnp.int32),
        pltpu.VMEM((LAYERS, 8, EMB, width), BF16),
        pltpu.VMEM((LAYERS + 1, 4, EMB, per), BF16),
        pltpu.VMEM((LAYERS, 4, EMB, width), F32),
        pltpu.VMEM((LAYERS, 4, EMB, width), F32),
        pltpu.VMEM((LAYERS, 4, EMB, width), F32),
        pltpu.VMEM((LAYERS, 2, HALF, width), F32),
        pltpu.VMEM((LAYERS, 4, HALF, width), F32),
        pltpu.VMEM((EMB, width), F32),
        pltpu.VMEM((EMB, per), F32),
        pltpu.VMEM((8, 8, width), F32),
        pltpu.VMEM((users, 128), F32),
        pltpu.VMEM((4, width), F32),
        pltpu.VMEM((4, width), F32),
        pltpu.VMEM((4, width), F32),
        pltpu.VMEM((3, 4, width), F32),
        pltpu.VMEM((4, width), F32),
        pltpu.VMEM((4, width), F32),
        pltpu.VMEM((8, users), F32),
        pltpu.VMEM((3, 8, users), F32),
        pltpu.VMEM((users, 128), F32),
        pltpu.VMEM((LAYERS, 4, EMB, per), F32),
        pltpu.VMEM((LAYERS, 3, EMB, per), F32),
        pltpu.VMEM((6, EMB, n_query), BF16),
        pltpu.SemaphoreType.DMA((STAGES,)),
        pltpu.SemaphoreType.DMA((N_COPIES,)),
        pltpu.SemaphoreType.DMA((N_COPIES,)),
    ]
    return pl.pallas_call(
        kernel,
        out_shape=(jax.ShapeDtypeStruct((EMB, per), BF16),
                   jax.ShapeDtypeStruct((EMB, width), BF16),
                   jax.ShapeDtypeStruct((EMB, n_query), BF16)),
        in_specs=[pl.BlockSpec(memory_space=pl.ANY), vmem, vmem, vmem],
        out_specs=(vmem, vmem, vmem),
        scratch_shapes=scratch,
        compiler_params=pltpu.CompilerParams(
            collective_id=0, has_side_effects=True, vmem_limit_bytes=67_000_000),
        name='propagate',
    )(mask_blk, item_shard, user_shard, queries.reshape(1, n_query))


def solution(mesh):
    def device_step(mask_blk, user_shard, item_shard, queries):
        fu_t, fi_t, picked_t = propagate(mask_blk, user_shard, item_shard, queries)
        scores = dot(picked_t, fi_t, TN)
        return fu_t.T, fi_t.T, scores

    return jax.shard_map(
        device_step, mesh=mesh,
        in_specs=(P('row', 'col'), P(('row', 'col'), None), P(('col', 'row'), None), P()),
        out_specs=(P(('row', 'col'), None), P(('col', 'row'), None), P(None, ('col', 'row'))),
        check_vma=False)
```

time: 460 us -> 129 us (0.28)
  waiting for transfers between devices: 250 us -> 0 us
  Pallas kernels: 0 us -> 120 us
  blocking collectives: 88.6 us -> 0 us
  matrix products: 64.8 us -> 2.79 us
  other arithmetic: 33.4 us -> 0 us
  between operations: 14.3 us -> 0.66 us
    reduce_scatter x6 -> x0, waiting for transfers between devices: 172 us -> none  [the longest x3 124 us: device_step(): lax.psum_scatter(item_part, 'row', scatter_dimension=0, tiled=True)]
    pallas_call x0 -> x1, Pallas kernels: none -> 120 us  [propagate(): pl.pallas_call(kernel, out_shape=(jax.ShapeDtypeStruct((EMB, per), BF16),...]
    dot_general x7 -> x1, matrix products: 64.8 us -> 2.79 us  [dot(): return lax.dot_general(lhs, rhs, dims, preferred_element_type=F32)]
    psum x2 -> x0, blocking collectives: 48.7 us -> none  [the longest x1 38.7 us: query_scores(): picked = lax.psum(picked, ('row', 'col'))]
    all_gather x3 -> x0, waiting for transfers between devices: 45.6 us -> none  [device_step(): item_panel = lax.all_gather(item_cur, 'row', axis=0, tiled=True)]
    all_gather x3 -> x0, blocking collectives: 39.8 us -> none  [device_step(): user_panel = lax.all_gather(user_cur, 'col', axis=0, tiled=True)]
    psum x1 -> x0, waiting for transfers between devices: 31.9 us -> none  [norm_block(): deg_item = lax.psum(jnp.sum(mask_blk, axis=0), 'row')]
    convert_element_type x6 -> x0, other arithmetic: 19.2 us -> none  [the longest x1 13.1 us: norm_block(): (inv_user[:, None] * mask_blk.astype(jnp.float32) * inv_item[None, :]).as...]
  transfers between devices with their start and end apart: 10 -> 0, of which waited for: 10 -> 0; matrix products, arithmetic and copies ran while one was open for 12% -> 0% of each run, Pallas kernels for 0% -> 0%
where the time goes in v1:
time: 129 us; the launch traced here: 128 us
  Pallas kernels  120 us (93%)
  local copies, waits for them, and re-layouts  4.7 us (4%)
  matrix products  2.79 us (2%)
    pallas_call x1, Pallas kernels, propagate(): pl.pallas_call(kernel, out_shape=(jax.ShapeDtypeStruct((EMB, per), BF16),...  120 us
    unnamed x8, local copies, waits for them, and re-layouts  4.7 us
    dot_general x1, matrix products, dot(): return lax.dot_general(lhs, rhs, dims, preferred_element_type=F32)  2.79 us

profile of v1, /device:TPU:0, one launch (start us, length us, event | category | flops | bytes accessed | tf_op | source)
XLA Modules:
  0.0 128.4 jit_solution(18100762314938984082)
XLA Ops:
  0.6 2.0 %copy.7.item_ref = bf16[2048,64]{1,0:T(8,128)(2,1)} copy(bf16[2048,64]{0,1:T(8,128)(2,1)} %param.6) | data formatting | bytes 524288 | tf_op args[2]
  2.6 1.4 %copy.8.user_ref = bf16[128,64]{1,0:T(8,128)(2,1)} copy(bf16[128,64]{0,1:T(8,128)(2,1)} %param.5) | data formatting | bytes 32768 | tf_op args[1]
  4.0 120.2 %propagate.1 = (bf16[64,128]{1,0:T(8,128)(2,1)}, bf16[64,2048]{1,0:T(8,128)(2,1)}, bf16[64,256]{1,0:T(8,128)(2,1)}) custom-call(s32[512,16384]{1,0:T(8,128)} %mask_ref.1, bf16[2048,64]{1,0:T(8,128)(2,1)} %copy.7.item_ref, bf16[128,64]{1,0:T(8,128)(2,1)} %copy.8.user_ref, s32[1,256]{1,0:T(1,128)} %bitcast.7), custom_call_target="tpu_custom_call" | custom-call | tf_op jit(solution)/shard_map/propagate/pallas_call | solution.py:344
  124.2 0.0 copy-start.1
  124.2 0.0 copy-start
  124.3 2.8 %fusion = f32[256,2048]{1,0:T(8,128)} fusion(bf16[64,256]{1,0:T(8,128)(2,1)} %get-tuple-element.8, bf16[64,2048]{1,0:T(8,128)(2,1)} %get-tuple-element.7), kind=kOutput, calls=%fused_computation | convolution fusion | flops 67108864 | bytes 2392064 | tf_op jit(solution)/shard_map/dot_general | solution.py:21
  127.0 0.0 copy-done.1
  127.1 0.6 copy.11
  127.7 0.0 copy-done
  127.7 0.7 copy.12
Async XLA Ops:
  124.2 2.8 %copy-start.1 = (bf16[64,128]{1,0:T(8,128)(2,1)S(1)}, bf16[64,128]{1,0:T(8,128)(2,1)}, u32[]{:S(2)}) copy-start(bf16[64,128]{1,0:T(8,128)(2,1)} %get-tuple-element.6) | copy-start | bytes 49156
  124.2 3.4 %copy-start = (bf16[64,2048]{1,0:T(8,128)(2,1)S(1)}, bf16[64,2048]{1,0:T(8,128)(2,1)}, u32[]{:S(2)}) copy-start(bf16[64,2048]{1,0:T(8,128)(2,1)} %get-tuple-element.7) | copy-start | bytes 786436

commit v2 on v1

v2 whole, which is shorter than its diff:
```python
import jax
import jax.numpy as jnp
from jax import lax
from jax.experimental import pallas as pl
from jax.experimental.pallas import tpu as pltpu
from jax.sharding import PartitionSpec as P

LAYERS = 3
EMB = 64
HALF = EMB // 2
NT = (((1,), (1,)), ((), ()))
NN = (((1,), (0,)), ((), ()))
TN = (((0,), (0,)), ((), ()))
F32 = jnp.float32
BF16 = jnp.bfloat16
STAGES = 4
N_COPIES = 112


def dot(lhs, rhs, dims):
    return lax.dot_general(lhs, rhs, dims, preferred_element_type=F32)


def kernel(mask_ref, item_ref, user_ref, query_ref, fu_ref, fi_ref, pick_ref,
           adj, stage, panel, upan, psend, drecv, sacc, hop1, rown, isum, usum,
           colacc, rowacc, deg_send, deg_recv, deg_own, deg_in, deg_fin, deg_oth,
           udeg, udeg_in, invu, uacc, upart, uin, pk, qbuf, stage_sem, in_sem, send_sem, recv_sem):
    c = lax.axis_index('col')
    r = lax.axis_index('row')
    users = rowacc.shape[0]
    width = adj.shape[2]
    rows = stage.shape[1]
    per_slot = users // rows
    core, cx, cy = r % 2, (r // 2) % 2, r // 4

    def plane(d, k):
        return ((cy + d // 2) % 2) * 4 + ((cx + d % 2) % 2) * 2 + (core + k) % 2

    def zpeer(k):
        return ((c // 2 + k // 2) % 2) * 2 + (c % 2 + k % 2) % 2

    slots = {d * 2 + k: (c, plane(d, k)) for d in range(4) for k in range(2)}
    partner, xn, yn, dg = slots[1], slots[2], slots[4], slots[6]
    zn = [None] + [(zpeer(k), r) for k in (1, 2, 3)]

    started = []

    def send(src, dst, device):
        n = len(started)
        copy = pltpu.make_async_remote_copy(
            src_ref=src, dst_ref=dst, send_sem=send_sem.at[n], recv_sem=recv_sem.at[n],
            device_id=device, device_id_type=pl.DeviceIdType.MESH)
        copy.start()
        started.append(copy)
        return copy

    def mask_copy(step):
        slot = step // per_slot
        part = step % per_slot
        col = plane(slot // 2, slot % 2) * width
        return pltpu.make_async_copy(
            mask_ref.at[pl.ds(pl.multiple_of(part * rows, rows), rows),
                        pl.ds(pl.multiple_of(col, width), width)],
            stage.at[step % STAGES], stage_sem.at[step % STAGES])

    steps = 8 * per_slot
    for s in range(STAGES):
        mask_copy(jnp.int32(s)).start()

    inputs = [pltpu.make_async_copy(item_ref, panel.at[0, 0], in_sem.at[0]),
              pltpu.make_async_copy(user_ref, upan.at[0, c], in_sem.at[1]),
              pltpu.make_async_copy(query_ref, qbuf, in_sem.at[2])]
    for copy in inputs:
        copy.start()

    barrier = pltpu.get_barrier_semaphore()
    peers = (partner, xn, yn, dg, zn[1], zn[2], zn[3])
    for device in peers:
        pl.semaphore_signal(barrier, inc=1, device_id=device, device_id_type=pl.DeviceIdType.MESH)

    rowacc[...] = jnp.zeros_like(rowacc)
    colacc[...] = jnp.zeros_like(colacc)

    def gather_start(n):
        own = panel.at[n, 0]
        lo, hi = pl.ds(0, HALF), pl.ds(HALF, HALF)
        g = {}
        g['xa'] = send(own.at[lo], panel.at[n, 2, lo], xn)
        g['yb'] = send(own.at[hi], panel.at[n, 4, hi], yn)
        g['xb'] = send(own.at[hi], panel.at[n, 2, hi], xn)
        g['ya'] = send(own.at[lo], panel.at[n, 4, lo], yn)
        g['p0'] = send(own, panel.at[n, 1], partner)
        return g

    def gather_forward(n, g):
        lo, hi = pl.ds(0, HALF), pl.ds(HALF, HALF)
        g['xa'].wait_recv()
        g['da'] = send(panel.at[n, 2, lo], panel.at[n, 6, lo], yn)
        g['yb'].wait_recv()
        g['db'] = send(panel.at[n, 4, hi], panel.at[n, 6, hi], xn)

    def gather_near(n, g):
        g['xb'].wait_recv()
        g['p1'] = send(panel.at[n, 2], panel.at[n, 3], partner)
        g['ya'].wait_recv()
        g['p2'] = send(panel.at[n, 4], panel.at[n, 5], partner)

    def gather_last(n, g):
        g['da'].wait_recv()
        g['db'].wait_recv()
        g['p3'] = send(panel.at[n, 6], panel.at[n, 7], partner)

    def zgather_start(n):
        return [send(upan.at[n, c], upan.at[n, c], zn[k]) for k in (1, 2, 3)]

    def zgather_wait(n, g):
        for copy in g:
            copy.wait_recv()
        return jnp.concatenate([upan[n, k] for k in range(4)], axis=1)

    def zsum_start(n, acc):
        acc_t = acc.T
        for k in range(4):
            upart[n, k] = acc_t[:, k * 128:(k + 1) * 128]
        return [send(upart.at[n, zpeer(k)], uin.at[n, k - 1], zn[k]) for k in (1, 2, 3)]

    def zsum_wait(n, g):
        for copy in g:
            copy.wait_recv()
        total = (upart[n, c] + uin[n, 0]) + (uin[n, 1] + uin[n, 2])
        nxt = total.astype(BF16)
        usum[...] = usum[...] + nxt.astype(F32)
        return nxt

    def mask_step(step, carry):
        mask_copy(step).wait()
        slot = step // per_slot
        part = step % per_slot
        buf = step % STAGES

        def group(i, col):
            at = pl.multiple_of(i * 16, 16)
            x = stage[buf, pl.ds(at, 16), :].astype(F32)
            row = pl.multiple_of(part * rows + i * 16, 16)
            adj[slot, pl.ds(row, 16), :] = x.astype(BF16)
            lanes = x[:, :128]
            for t in range(1, width // 128):
                lanes = lanes + x[:, t * 128:(t + 1) * 128]
            rowacc[pl.ds(row, 16), :] += lanes
            return col + (x[:8] + x[8:])

        colacc[slot] += lax.fori_loop(0, rows // 16, group, jnp.zeros((8, width), F32), unroll=2)

        @pl.when(step + STAGES < steps)
        def _():
            mask_copy(step + STAGES).start()

        return carry

    with jax.named_scope('mask_a'):
        lax.fori_loop(0, steps * 3 // 8, mask_step, 0)
    with jax.named_scope('barrier'):
        pl.semaphore_wait(barrier, len(peers))
    with jax.named_scope('inputs'):
        for copy in inputs:
            copy.wait()
        gather0 = gather_start(0)
        zgather0 = zgather_start(0)
        isum[...] = panel[0, 0].astype(F32)
        usum[...] = upan[0, c].astype(F32)
    with jax.named_scope('mask_b'):
        lax.fori_loop(steps * 3 // 8, steps, mask_step, 0)

    with jax.named_scope('degrees'):
        for d in range(4):
            deg_send[d:d + 1, :] = jnp.sum(colacc[2 * d + 1], axis=0, keepdims=True)
        dp = send(deg_send, deg_recv, partner)
        udeg[...] = dot(jnp.ones((8, 128), BF16), rowacc[...].astype(BF16), NT)
        zd = [send(udeg, udeg_in.at[k - 1], zn[k]) for k in (1, 2, 3)]
        mine = jnp.concatenate(
            [jnp.sum(colacc[2 * d], axis=0, keepdims=True) for d in range(4)], axis=0)
        gather_forward(0, gather0)
        dp.wait_recv()
        deg_own[...] = mine + deg_recv[...]
        ds = [send(deg_own, deg_in.at[0], xn), send(deg_own, deg_in.at[1], yn),
              send(deg_own, deg_in.at[2], dg)]
        gather_near(0, gather0)
        for copy in zd:
            copy.wait_recv()
        du = (udeg[...] + udeg_in[0]) + (udeg_in[1] + udeg_in[2])
        inv = lax.rsqrt(jnp.maximum(du, 1.0))
        invu[...] = jnp.broadcast_to(inv[0:1, :], (128, users)).T
        for copy in ds:
            copy.wait_recv()
        for d in range(4):
            total = ((deg_own[d:d + 1, :] + deg_in[0, (d ^ 1):(d ^ 1) + 1, :])
                     + (deg_in[1, (d ^ 2):(d ^ 2) + 1, :] + deg_in[2, (d ^ 3):(d ^ 3) + 1, :]))
            deg_fin[d:d + 1, :] = lax.rsqrt(jnp.maximum(total, 1.0))
        df = send(deg_fin, deg_oth, partner)

    def normalize(slot):
        d = slot // 2
        inv_item = (deg_oth if slot % 2 else deg_fin)[d:d + 1, :]

        def group(i, carry):
            at = pl.multiple_of(i * 16, 16)
            inv_user = jnp.concatenate([invu[pl.ds(at, 16), :]] * (width // 128), axis=1)
            adj[slot, pl.ds(at, 16), :] = adj[slot, pl.ds(at, 16), :] * (inv_user * inv_item).astype(BF16)
            return carry

        lax.fori_loop(0, users // 16, group, 0, unroll=2)

    def items_out(n, d, s):
        lo, hi = pl.ds(0, HALF), pl.ds(HALF, HALF)
        if d == 3:
            s['x1'] = send(sacc.at[n, 3, lo], hop1.at[n, 0], xn)
            s['y1'] = send(sacc.at[n, 3, hi], hop1.at[n, 1], yn)
        elif d == 1:
            s['xa'] = send(sacc.at[n, 1, lo], rown.at[n, 0], xn)
        else:
            s['yb'] = send(sacc.at[n, 2, hi], rown.at[n, 3], yn)

    def items_start(n, u, first=False):
        p, s = {}, {}

        def away(d):
            if first:
                normalize(2 * d + 1)
            psend[n, d] = dot(u, adj[2 * d + 1], NN)
            p[d] = send(psend.at[n, d], drecv.at[n, d], partner)

        def near(d):
            if first:
                normalize(2 * d)
            part = dot(u, adj[2 * d], NN)
            if d:
                p[d].wait_recv()
                part = part + drecv[n, d]
            sacc[n, d] = part

        away(3)
        away(1)
        near(3)
        if first:
            items_out(n, 3, s)
        away(2)
        near(1)
        if first:
            items_out(n, 1, s)
        away(0)
        near(2)
        if first:
            items_out(n, 2, s)
        near(0)
        s['p'] = p[0]
        return s

    def items_send(n, s):
        for d in (3, 1, 2):
            items_out(n, d, s)

    def items_mid(n, s):
        lo, hi = pl.ds(0, HALF), pl.ds(HALF, HALF)
        s['x1'].wait_recv()
        sacc[n, 2, lo] = sacc[n, 2, lo] + hop1[n, 0]
        s['ya'] = send(sacc.at[n, 2, lo], rown.at[n, 2], yn)
        s['y1'].wait_recv()
        sacc[n, 1, hi] = sacc[n, 1, hi] + hop1[n, 1]
        s['xb'] = send(sacc.at[n, 1, hi], rown.at[n, 1], xn)

    def items_finish(n, s):
        for key in ('p', 'xa', 'yb', 'ya', 'xb'):
            s[key].wait_recv()
        for h, at in ((0, pl.ds(0, HALF)), (1, pl.ds(HALF, HALF))):
            total = ((sacc[n, 0, at] + drecv[n, 0, at]) + rown[n, h]) + rown[n, 2 + h]
            nxt = total.astype(BF16)
            isum[at] = isum[at] + nxt.astype(F32)
            if n + 1 < LAYERS:
                panel[n + 1, 0, at] = nxt

    def user_partial(n, g, near=True, hook=None):
        def slots(first, stride, count):
            def one(j, carry):
                at = first + stride * j
                uacc[...] += dot(adj[at], panel[n, at], NT)
                return carry

            lax.fori_loop(0, count, one, 0)

        g['p0'].wait_recv()
        uacc[...] = dot(adj[0], panel[n, 0], NT)
        slots(1, 1, 1)
        if hook is not None:
            hook()
        if near:
            gather_near(n, g)
        slots(2, 2, 2)
        g['p1'].wait_recv()
        g['p2'].wait_recv()
        slots(3, 2, 2)
        gather_last(n, g)
        slots(6, 1, 1)
        g['p3'].wait_recv()
        slots(7, 1, 1)
        return uacc[...]

    scope = jax.named_scope
    with scope('u0'):
        u0 = zgather_wait(0, zgather0)
        df.wait_recv()
    with scope('items0'):
        s0 = items_start(0, u0, first=True)
    with scope('user0'):
        z0 = zsum_start(0, user_partial(0, gather0, near=False))
    with scope('mid0'):
        items_mid(0, s0)
    with scope('zsum0'):
        upan[1, c] = zsum_wait(0, z0)
        zg1 = zgather_start(1)
    with scope('finish0'):
        items_finish(0, s0)
        g1 = gather_start(1)
    with scope('zgather1'):
        u1 = zgather_wait(1, zg1)
    with scope('items1'):
        s1 = items_start(1, u1)
        gather_forward(1, g1)
        items_send(1, s1)
    with scope('user1'):
        z1 = zsum_start(1, user_partial(1, g1))
    with scope('zsum1'):
        upan[2, c] = zsum_wait(1, z1)
        zg2 = zgather_start(2)
    with scope('mid1'):
        items_mid(1, s1)
    with scope('zgather2'):
        u2 = zgather_wait(2, zg2)
    with scope('items2'):
        s2 = items_start(2, u2)
    with scope('finish1'):
        items_finish(1, s1)
        g2 = gather_start(2)
    with scope('user2'):
        def hook():
            gather_forward(2, g2)
            items_send(2, s2)

        z2 = zsum_start(2, user_partial(2, g2, hook=hook))
    with scope('mid2'):
        items_mid(2, s2)
    with scope('zsum2'):
        zsum_wait(2, z2)
        final_user = (usum[...] / (LAYERS + 1)).astype(BF16)
        fu_ref[...] = final_user
        upan[3, c] = final_user
        zg3 = zgather_start(3)
    with scope('zgather3'):
        ufin = zgather_wait(3, zg3)
    with scope('pick'):
        local = qbuf[...] - r * users
        chosen = (lax.broadcasted_iota(jnp.int32, (users, local.shape[1]), 0)
                  == jnp.broadcast_to(local, (users, local.shape[1]))).astype(F32).astype(BF16)
        pk[0] = dot(ufin, chosen, NN).astype(BF16)
        q = send(pk.at[0], pk.at[1], partner)
        q.wait_recv()
        pk[2] = pk[0] + pk[1]
        qs = [send(pk.at[2], pk.at[3 + i], dev) for i, dev in enumerate((xn, yn, dg))]
    with scope('finish2'):
        items_finish(2, s2)
        fi_ref[...] = (isum[...] / (LAYERS + 1)).astype(BF16)
    with scope('picked'):
        for copy in qs:
            copy.wait_recv()
        pick_ref[...] = (pk[2] + pk[3]) + (pk[4] + pk[5])
    with scope('drain'):
        for copy in started:
            copy.wait_send()


def propagate(mask_blk, user_shard, item_shard, queries):
    users, items = mask_blk.shape
    width = items // 8
    per = user_shard.shape[1]
    n_query = queries.shape[0]
    vmem = pl.BlockSpec(memory_space=pltpu.VMEM)
    hbm = pl.BlockSpec(memory_space=pl.ANY)
    scratch = [
        pltpu.VMEM((8, users, width), BF16),
        pltpu.VMEM((STAGES, users // 2, width), jnp.int32),
        pltpu.VMEM((LAYERS, 8, EMB, width), BF16),
        pltpu.VMEM((LAYERS + 1, 4, EMB, per), BF16),
        pltpu.VMEM((LAYERS, 4, EMB, width), F32),
        pltpu.VMEM((LAYERS, 4, EMB, width), F32),
        pltpu.VMEM((LAYERS, 4, EMB, width), F32),
        pltpu.VMEM((LAYERS, 2, HALF, width), F32),
        pltpu.VMEM((LAYERS, 4, HALF, width), F32),
        pltpu.VMEM((EMB, width), F32),
        pltpu.VMEM((EMB, per), F32),
        pltpu.VMEM((8, 8, width), F32),
        pltpu.VMEM((users, 128), F32),
        pltpu.VMEM((4, width), F32),
        pltpu.VMEM((4, width), F32),
        pltpu.VMEM((4, width), F32),
        pltpu.VMEM((3, 4, width), F32),
        pltpu.VMEM((4, width), F32),
        pltpu.VMEM((4, width), F32),
        pltpu.VMEM((8, users), F32),
        pltpu.VMEM((3, 8, users), F32),
        pltpu.VMEM((users, 128), F32),
        pltpu.VMEM((users, EMB), F32),
        pltpu.VMEM((LAYERS, 4, EMB, per), F32),
        pltpu.VMEM((LAYERS, 3, EMB, per), F32),
        pltpu.VMEM((6, EMB, n_query), BF16),
        pltpu.VMEM((1, n_query), jnp.int32),
        pltpu.SemaphoreType.DMA((STAGES,)),
        pltpu.SemaphoreType.DMA((3,)),
        pltpu.SemaphoreType.DMA((N_COPIES,)),
        pltpu.SemaphoreType.DMA((N_COPIES,)),
    ]
    return pl.pallas_call(
        kernel,
        out_shape=(jax.ShapeDtypeStruct((EMB, per), BF16),
                   jax.ShapeDtypeStruct((EMB, width), BF16),
                   jax.ShapeDtypeStruct((EMB, n_query), BF16)),
        in_specs=[hbm, hbm, hbm, hbm],
        out_specs=(vmem, vmem, vmem),
        scratch_shapes=scratch,
        compiler_params=pltpu.CompilerParams(
            collective_id=0, has_side_effects=True, vmem_limit_bytes=67_000_000),
        name='propagate',
    )(mask_blk, item_shard, user_shard, queries.reshape(1, n_query))


def solution(mesh):
    def device_step(mask_blk, user_shard, item_shard, queries):
        fu_t, fi_t, picked_t = propagate(mask_blk, user_shard.T, item_shard.T, queries)
        scores = dot(picked_t, fi_t, TN)
        return fu_t.T, fi_t.T, scores

    return jax.shard_map(
        device_step, mesh=mesh,
        in_specs=(P('row', 'col'), P(('row', 'col'), None), P(('col', 'row'), None), P()),
        out_specs=(P(('row', 'col'), None), P(('col', 'row'), None), P(None, ('col', 'row'))),
        check_vma=False)
```

time: 129 us -> 108 us (0.84)
  Pallas kernels: 120 us -> 104 us
  local copies, waits for them, and re-layouts: 4.7 us -> 1.32 us
    pallas_call x1, Pallas kernels: 120 us -> 104 us  [propagate(): pl.pallas_call(kernel, out_shape=(jax.ShapeDtypeStruct((EMB, per), BF16),...]
    unnamed x8 -> x6, local copies, waits for them, and re-layouts: 4.7 us -> 1.32 us
where the time goes in v2:
time: 108 us
  Pallas kernels  104 us (96%)
  matrix products  2.79 us (3%)
  local copies, waits for them, and re-layouts  1.32 us (1%)
    pallas_call x1, Pallas kernels, propagate(): pl.pallas_call(kernel, out_shape=(jax.ShapeDtypeStruct((EMB, per), BF16),...  104 us
    dot_general x1, matrix products, dot(): return lax.dot_general(lhs, rhs, dims, preferred_element_type=F32)  2.79 us

profile of v2, /device:TPU:0, one launch (start us, length us, event | category | flops | bytes accessed | tf_op | source)
XLA Modules:
  0.0 108.3 jit_solution(13179217664528577094)
XLA Ops:
  0.6 103.5 %propagate.1 = (bf16[64,128]{1,0:T(8,128)(2,1)}, bf16[64,2048]{1,0:T(8,128)(2,1)}, bf16[64,256]{1,0:T(8,128)(2,1)}) custom-call(s32[512,16384]{1,0:T(8,128)} %mask_ref.1, bf16[64,2048]{1,0:T(8,128)(2,1)} %bitcast.8, bf16[64,128]{1,0:T(8,128)(2,1)} %bitcast.9, s32[1,256]{1,0:T(1,128)} %bitcast.11), custom_call_target="tpu_custom_call" | custom-call | tf_op jit(solution)/shard_map/propagate/pallas_call | solution.py:420
  104.2 0.0 copy-start.1
  104.2 0.0 copy-start
  104.2 2.8 %fusion = f32[256,2048]{1,0:T(8,128)} fusion(bf16[64,256]{1,0:T(8,128)(2,1)} %get-tuple-element.8, bf16[64,2048]{1,0:T(8,128)(2,1)} %get-tuple-element.7), kind=kOutput, calls=%fused_computation | convolution fusion | flops 67108864 | bytes 2392064 | tf_op jit(solution)/shard_map/dot_general | solution.py:21
  107.0 0.0 copy-done.1
  107.0 0.6 copy.9
  107.6 0.0 copy-done
  107.6 0.7 copy.10
Async XLA Ops:
  104.2 2.8 %copy-start.1 = (bf16[64,128]{1,0:T(8,128)(2,1)S(1)}, bf16[64,128]{1,0:T(8,128)(2,1)}, u32[]{:S(2)}) copy-start(bf16[64,128]{1,0:T(8,128)(2,1)} %get-tuple-element.6) | copy-start | bytes 49156
  104.2 3.4 %copy-start = (bf16[64,2048]{1,0:T(8,128)(2,1)S(1)}, bf16[64,2048]{1,0:T(8,128)(2,1)}, u32[]{:S(2)}) copy-start(bf16[64,2048]{1,0:T(8,128)(2,1)} %get-tuple-element.7) | copy-start | bytes 786436

commit v3 on v2

--- a/solution.py
+++ b/solution.py
@@ -8,13 +8,14 @@
 LAYERS = 3
 EMB = 64
 HALF = EMB // 2
+QUARTER = EMB // 4
 NT = (((1,), (1,)), ((), ()))
 NN = (((1,), (0,)), ((), ()))
 TN = (((0,), (0,)), ((), ()))
 F32 = jnp.float32
 BF16 = jnp.bfloat16
-STAGES = 4
-N_COPIES = 112
+STAGES = 8
+N_COPIES = 160
 
 
 def dot(lhs, rhs, dims):
@@ -23,7 +24,7 @@
 
 def kernel(mask_ref, item_ref, user_ref, query_ref, fu_ref, fi_ref, pick_ref,
            adj, stage, panel, upan, psend, drecv, sacc, hop1, rown, isum, usum,
-           colacc, rowacc, deg_send, deg_recv, deg_own, deg_in, deg_fin, deg_oth,
+           colacc, rowacc, deg_send, deg_recv, deg_own, deg_in, deg_fin, deg_oth, far_send, far_in,
            udeg, udeg_in, invu, uacc, upart, uin, pk, qbuf, stage_sem, in_sem, send_sem, recv_sem):
     c = lax.axis_index('col')
     r = lax.axis_index('row')
@@ -54,8 +55,11 @@
         started.append(copy)
         return copy
 
+    def mask_slot(step):
+        return (step // per_slot % 4) * 2 + 1 - step // (4 * per_slot)
+
     def mask_copy(step):
-        slot = step // per_slot
+        slot = mask_slot(step)
         part = step % per_slot
         col = plane(slot // 2, slot % 2) * width
         return pltpu.make_async_copy(
@@ -74,44 +78,46 @@
         copy.start()
 
     barrier = pltpu.get_barrier_semaphore()
-    peers = (partner, xn, yn, dg, zn[1], zn[2], zn[3])
+    peers = tuple(slots[k] for k in range(1, 8)) + (zn[1], zn[2], zn[3])
     for device in peers:
         pl.semaphore_signal(barrier, inc=1, device_id=device, device_id_type=pl.DeviceIdType.MESH)
 
     rowacc[...] = jnp.zeros_like(rowacc)
     colacc[...] = jnp.zeros_like(colacc)
 
-    def gather_start(n):
+    def piece(h, i):
+        return pl.ds(h * HALF + i * QUARTER, QUARTER)
+
+    def gather_start(n, i, g):
         own = panel.at[n, 0]
-        lo, hi = pl.ds(0, HALF), pl.ds(HALF, HALF)
-        g = {}
-        g['xa'] = send(own.at[lo], panel.at[n, 2, lo], xn)
-        g['yb'] = send(own.at[hi], panel.at[n, 4, hi], yn)
-        g['xb'] = send(own.at[hi], panel.at[n, 2, hi], xn)
-        g['ya'] = send(own.at[lo], panel.at[n, 4, lo], yn)
-        g['p0'] = send(own, panel.at[n, 1], partner)
-        return g
-
-    def gather_forward(n, g):
-        lo, hi = pl.ds(0, HALF), pl.ds(HALF, HALF)
-        g['xa'].wait_recv()
-        g['da'] = send(panel.at[n, 2, lo], panel.at[n, 6, lo], yn)
-        g['yb'].wait_recv()
-        g['db'] = send(panel.at[n, 4, hi], panel.at[n, 6, hi], xn)
+        for h in (0, 1):
+            g['x', h, i] = send(own.at[piece(h, i)], panel.at[n, 2, piece(h, i)], xn)
+            g['y', 1 - h, i] = send(own.at[piece(1 - h, i)], panel.at[n, 4, piece(1 - h, i)], yn)
+        if i:
+            g['p0'] = send(own, panel.at[n, 1], partner)
+
+    def gather_forward(n, i, g):
+        g['x', 0, i].wait_recv()
+        g['d', 0, i] = send(panel.at[n, 2, piece(0, i)], panel.at[n, 6, piece(0, i)], yn)
+        g['y', 1, i].wait_recv()
+        g['d', 1, i] = send(panel.at[n, 4, piece(1, i)], panel.at[n, 6, piece(1, i)], xn)
 
     def gather_near(n, g):
-        g['xb'].wait_recv()
+        g['x', 1, 0].wait_recv()
+        g['x', 1, 1].wait_recv()
         g['p1'] = send(panel.at[n, 2], panel.at[n, 3], partner)
-        g['ya'].wait_recv()
+        g['y', 0, 0].wait_recv()
+        g['y', 0, 1].wait_recv()
         g['p2'] = send(panel.at[n, 4], panel.at[n, 5], partner)
 
     def gather_last(n, g):
-        g['da'].wait_recv()
-        g['db'].wait_recv()
+        for h in (0, 1):
+            for i in (0, 1):
+                g['d', h, i].wait_recv()
         g['p3'] = send(panel.at[n, 6], panel.at[n, 7], partner)
 
     def zgather_start(n):
-        return [send(upan.at[n, c], upan.at[n, c], zn[k]) for k in (1, 2, 3)]
+        return [send(upan.at[n, c], upan.at[n, c], zn[k]) for k in (3, 2, 1)]
 
     def zgather_wait(n, g):
         for copy in g:
@@ -122,7 +128,7 @@
         acc_t = acc.T
         for k in range(4):
             upart[n, k] = acc_t[:, k * 128:(k + 1) * 128]
-        return [send(upart.at[n, zpeer(k)], uin.at[n, k - 1], zn[k]) for k in (1, 2, 3)]
+        return [send(upart.at[n, zpeer(k)], uin.at[n, k - 1], zn[k]) for k in (3, 2, 1)]
 
     def zsum_wait(n, g):
         for copy in g:
@@ -134,7 +140,7 @@
 
     def mask_step(step, carry):
         mask_copy(step).wait()
-        slot = step // per_slot
+        slot = mask_slot(step)
         part = step % per_slot
         buf = step % STAGES
 
@@ -158,70 +164,92 @@
         return carry
 
     with jax.named_scope('mask_a'):
-        lax.fori_loop(0, steps * 3 // 8, mask_step, 0)
+        lax.fori_loop(0, steps // 4, mask_step, 0)
     with jax.named_scope('barrier'):
         pl.semaphore_wait(barrier, len(peers))
     with jax.named_scope('inputs'):
         for copy in inputs:
             copy.wait()
-        gather0 = gather_start(0)
+        g0 = {}
+        gather_start(0, 0, g0)
+        gather_start(0, 1, g0)
         zgather0 = zgather_start(0)
         isum[...] = panel[0, 0].astype(F32)
         usum[...] = upan[0, c].astype(F32)
     with jax.named_scope('mask_b'):
-        lax.fori_loop(steps * 3 // 8, steps, mask_step, 0)
-
-    with jax.named_scope('degrees'):
+        lax.fori_loop(steps // 4, steps * 5 // 8, mask_step, 0)
         for d in range(4):
             deg_send[d:d + 1, :] = jnp.sum(colacc[2 * d + 1], axis=0, keepdims=True)
         dp = send(deg_send, deg_recv, partner)
+    with jax.named_scope('mask_c'):
+        lax.fori_loop(steps * 5 // 8, steps, mask_step, 0)
+
+    with jax.named_scope('deg_sum'):
         udeg[...] = dot(jnp.ones((8, 128), BF16), rowacc[...].astype(BF16), NT)
-        zd = [send(udeg, udeg_in.at[k - 1], zn[k]) for k in (1, 2, 3)]
+        zd = [send(udeg, udeg_in.at[k - 1], zn[k]) for k in (3, 2, 1)]
         mine = jnp.concatenate(
             [jnp.sum(colacc[2 * d], axis=0, keepdims=True) for d in range(4)], axis=0)
-        gather_forward(0, gather0)
+    with jax.named_scope('deg_partner'):
         dp.wait_recv()
         deg_own[...] = mine + deg_recv[...]
         ds = [send(deg_own, deg_in.at[0], xn), send(deg_own, deg_in.at[1], yn),
               send(deg_own, deg_in.at[2], dg)]
-        gather_near(0, gather0)
+        far = []
+        for d in range(4):
+            far_send[d] = deg_own[d:d + 1, :]
+            far.append(send(far_send.at[d], far_in.at[d], slots[2 * (3 - d) + 1]))
+    with jax.named_scope('deg_users'):
         for copy in zd:
             copy.wait_recv()
         du = (udeg[...] + udeg_in[0]) + (udeg_in[1] + udeg_in[2])
         inv = lax.rsqrt(jnp.maximum(du, 1.0))
         invu[...] = jnp.broadcast_to(inv[0:1, :], (128, users)).T
+    with jax.named_scope('deg_items'):
         for copy in ds:
             copy.wait_recv()
+    with jax.named_scope('deg_inv'):
         for d in range(4):
             total = ((deg_own[d:d + 1, :] + deg_in[0, (d ^ 1):(d ^ 1) + 1, :])
                      + (deg_in[1, (d ^ 2):(d ^ 2) + 1, :] + deg_in[2, (d ^ 3):(d ^ 3) + 1, :]))
             deg_fin[d:d + 1, :] = lax.rsqrt(jnp.maximum(total, 1.0))
         df = send(deg_fin, deg_oth, partner)
-
-    def normalize(slot):
+        for copy in far:
+            copy.wait_recv()
+        for i in (0, 1):
+            gather_forward(0, i, g0)
+        gather_near(0, g0)
+
+    def normalize(slot, at=0, size=width):
         d = slot // 2
-        inv_item = (deg_oth if slot % 2 else deg_fin)[d:d + 1, :]
+        cols = pl.ds(at, size)
+        if slot == 7:
+            total = (far_in[3, :, cols] + far_in[2, :, cols]) + (far_in[1, :, cols] + far_in[0, :, cols])
+            inv_item = lax.rsqrt(jnp.maximum(total, 1.0))
+        else:
+            inv_item = (deg_oth if slot % 2 else deg_fin)[d:d + 1, cols]
 
         def group(i, carry):
-            at = pl.multiple_of(i * 16, 16)
-            inv_user = jnp.concatenate([invu[pl.ds(at, 16), :]] * (width // 128), axis=1)
-            adj[slot, pl.ds(at, 16), :] = adj[slot, pl.ds(at, 16), :] * (inv_user * inv_item).astype(BF16)
+            row = pl.ds(pl.multiple_of(i * 16, 16), 16)
+            inv_user = jnp.concatenate([invu[row, :]] * (size // 128), axis=1)
+            adj[slot, row, cols] = adj[slot, row, cols] * (inv_user * inv_item).astype(BF16)
             return carry
 
         lax.fori_loop(0, users // 16, group, 0, unroll=2)
 
-    def items_out(n, d, s):
+    halves = (pl.ds(0, width // 2), pl.ds(width // 2, width // 2))
+
+    def items_diagonal(n, i, s):
+        cols = halves[i]
         lo, hi = pl.ds(0, HALF), pl.ds(HALF, HALF)
-        if d == 3:
-            s['x1'] = send(sacc.at[n, 3, lo], hop1.at[n, 0], xn)
-            s['y1'] = send(sacc.at[n, 3, hi], hop1.at[n, 1], yn)
-        elif d == 1:
-            s['xa'] = send(sacc.at[n, 1, lo], rown.at[n, 0], xn)
-        else:
-            s['yb'] = send(sacc.at[n, 2, hi], rown.at[n, 3], yn)
-
-    def items_start(n, u, first=False):
-        p, s = {}, {}
+        s['x1', i] = send(sacc.at[n, 3, lo, cols], hop1.at[n, 0, :, cols], xn)
+        s['y1', i] = send(sacc.at[n, 3, hi, cols], hop1.at[n, 1, :, cols], yn)
+
+    def items_direct(n, s):
+        s['xa'] = send(sacc.at[n, 1, pl.ds(0, HALF)], rown.at[n, 0], xn)
+        s['yb'] = send(sacc.at[n, 2, pl.ds(HALF, HALF)], rown.at[n, 3], yn)
+
+    def items_start(n, u, s, first=False, hooks=()):
+        p = {}
 
         def away(d):
             if first:
@@ -238,45 +266,66 @@
                 part = part + drecv[n, d]
             sacc[n, d] = part
 
-        away(3)
-        away(1)
-        near(3)
         if first:
-            items_out(n, 3, s)
-        away(2)
-        near(1)
-        if first:
-            items_out(n, 1, s)
-        away(0)
-        near(2)
-        if first:
-            items_out(n, 2, s)
-        near(0)
+            for i, cols in enumerate(halves):
+                normalize(7, i * (width // 2), width // 2)
+                psend[n, 3, :, cols] = dot(u, adj[7, :, cols], NN)
+                p[3, i] = send(psend.at[n, 3, :, cols], drecv.at[n, 3, :, cols], partner)
+            for i, cols in enumerate(halves):
+                normalize(6, i * (width // 2), width // 2)
+                own = dot(u, adj[6, :, cols], NN)
+                p[3, i].wait_recv()
+                sacc[n, 3, :, cols] = own + drecv[n, 3, :, cols]
+                items_diagonal(n, i, s)
+            df.wait_recv()
+            away(1)
+            away(2)
+            near(1)
+            s['xa'] = send(sacc.at[n, 1, pl.ds(0, HALF)], rown.at[n, 0], xn)
+            away(0)
+            near(2)
+            s['yb'] = send(sacc.at[n, 2, pl.ds(HALF, HALF)], rown.at[n, 3], yn)
+            near(0)
+        else:
+            away(3)
+            away(1)
+            hooks[0]()
+            near(3)
+            hooks[1]()
+            away(2)
+            away(0)
+            near(1)
+            hooks[2]()
+            near(2)
+            near(0)
+            hooks[3]()
         s['p'] = p[0]
-        return s
-
-    def items_send(n, s):
-        for d in (3, 1, 2):
-            items_out(n, d, s)
 
     def items_mid(n, s):
-        lo, hi = pl.ds(0, HALF), pl.ds(HALF, HALF)
-        s['x1'].wait_recv()
-        sacc[n, 2, lo] = sacc[n, 2, lo] + hop1[n, 0]
-        s['ya'] = send(sacc.at[n, 2, lo], rown.at[n, 2], yn)
-        s['y1'].wait_recv()
-        sacc[n, 1, hi] = sacc[n, 1, hi] + hop1[n, 1]
-        s['xb'] = send(sacc.at[n, 1, hi], rown.at[n, 1], xn)
-
-    def items_finish(n, s):
-        for key in ('p', 'xa', 'yb', 'ya', 'xb'):
-            s[key].wait_recv()
-        for h, at in ((0, pl.ds(0, HALF)), (1, pl.ds(HALF, HALF))):
-            total = ((sacc[n, 0, at] + drecv[n, 0, at]) + rown[n, h]) + rown[n, 2 + h]
+        for i in (0, 1):
+            s['x1', i].wait_recv()
+            s['y1', i].wait_recv()
+        for i in (0, 1):
+            at = pl.ds(i * QUARTER, QUARTER)
+            sacc[n, 2, piece(0, i)] = sacc[n, 2, piece(0, i)] + hop1[n, 0, at]
+            s['ya', i] = send(sacc.at[n, 2, piece(0, i)], rown.at[n, 2, at], yn)
+            sacc[n, 1, piece(1, i)] = sacc[n, 1, piece(1, i)] + hop1[n, 1, at]
+            s['xb', i] = send(sacc.at[n, 1, piece(1, i)], rown.at[n, 1, at], xn)
+
+    def items_finish(n, i, s):
+        if i == 0:
+            for key in ('p', 'xa', 'yb'):
+                s[key].wait_recv()
+        s['ya', i].wait_recv()
+        s['xb', i].wait_recv()
+        at = pl.ds(i * QUARTER, QUARTER)
+        for h in (0, 1):
+            rows_h = piece(h, i)
+            total = ((sacc[n, 0, rows_h] + drecv[n, 0, rows_h]) + rown[n, h, at]) + rown[n, 2 + h, at]
             nxt = total.astype(BF16)
-            isum[at] = isum[at] + nxt.astype(F32)
+            isum[rows_h] = isum[rows_h] + nxt.astype(F32)
             if n + 1 < LAYERS:
-                panel[n + 1, 0, at] = nxt
+                panel[n + 1, 0, rows_h] = nxt
 
     def user_partial(n, g, near=True, hook=None):
         def slots(first, stride, count):
@@ -290,14 +339,14 @@
         g['p0'].wait_recv()
         uacc[...] = dot(adj[0], panel[n, 0], NT)
         slots(1, 1, 1)
-        if hook is not None:
-            hook()
         if near:
             gather_near(n, g)
         slots(2, 2, 2)
         g['p1'].wait_recv()
         g['p2'].wait_recv()
         slots(3, 2, 2)
+        if hook is not None:
+            hook()
         gather_last(n, g)
         slots(6, 1, 1)
         g['p3'].wait_recv()
@@ -305,47 +354,63 @@
         return uacc[...]
 
     scope = jax.named_scope
+
+    def finish(n, i, s, g):
+        with scope(f'finish{n}{i}'):
+            items_finish(n, i, s)
+            gather_start(n + 1, i, g)
+
+    def forward(n, i, g):
+        with scope(f'forward{n}{i}'):
+            gather_forward(n, i, g)
+
+    def nothing():
+        pass
+
     with scope('u0'):
         u0 = zgather_wait(0, zgather0)
-        df.wait_recv()
     with scope('items0'):
-        s0 = items_start(0, u0, first=True)
+        s0 = {}
+        items_start(0, u0, s0, first=True)
     with scope('user0'):
-        z0 = zsum_start(0, user_partial(0, gather0, near=False))
-    with scope('mid0'):
-        items_mid(0, s0)
+        z0 = zsum_start(0, user_partial(0, g0, near=False, hook=lambda: items_mid(0, s0)))
+    g1, g2 = {}, {}
+    finish(0, 0, s0, g1)
     with scope('zsum0'):
         upan[1, c] = zsum_wait(0, z0)
         zg1 = zgather_start(1)
-    with scope('finish0'):
-        items_finish(0, s0)
-        g1 = gather_start(1)
+    finish(0, 1, s0, g1)
     with scope('zgather1'):
         u1 = zgather_wait(1, zg1)
     with scope('items1'):
-        s1 = items_start(1, u1)
-        gather_forward(1, g1)
-        items_send(1, s1)
+        def launch1():
+            forward(1, 1, g1)
+            items_diagonal(1, 0, s1)
+            items_diagonal(1, 1, s1)
+
+        forward(1, 0, g1)
+        s1 = {}
+        items_start(1, u1, s1, hooks=(nothing, launch1, nothing, nothing))
+        items_direct(1, s1)
     with scope('user1'):
         z1 = zsum_start(1, user_partial(1, g1))
+    with scope('mid1'):
+        items_mid(1, s1)
     with scope('zsum1'):
         upan[2, c] = zsum_wait(1, z1)
         zg2 = zgather_start(2)
-    with scope('mid1'):
-        items_mid(1, s1)
     with scope('zgather2'):
         u2 = zgather_wait(2, zg2)
     with scope('items2'):
-        s2 = items_start(2, u2)
-    with scope('finish1'):
-        items_finish(1, s1)
-        g2 = gather_start(2)
+        s2 = {}
+        items_start(2, u2, s2, hooks=(lambda: finish(1, 0, s1, g2), lambda: finish(1, 1, s1, g2),
+                                      lambda: forward(2, 0, g2), nothing))
+        forward(2, 1, g2)
+        items_diagonal(2, 0, s2)
+        items_diagonal(2, 1, s2)
+        items_direct(2, s2)
     with scope('user2'):
-        def hook():
-            gather_forward(2, g2)
-            items_send(2, s2)
-
-        z2 = zsum_start(2, user_partial(2, g2, hook=hook))
+        z2 = zsum_start(2, user_partial(2, g2))
     with scope('mid2'):
         items_mid(2, s2)
     with scope('zsum2'):
@@ -366,7 +431,8 @@
         pk[2] = pk[0] + pk[1]
         qs = [send(pk.at[2], pk.at[3 + i], dev) for i, dev in enumerate((xn, yn, dg))]
     with scope('finish2'):
-        items_finish(2, s2)
+        items_finish(2, 0, s2)
+        items_finish(2, 1, s2)
         fi_ref[...] = (isum[...] / (LAYERS + 1)).astype(BF16)
     with scope('picked'):
         for copy in qs:
@@ -386,7 +452,7 @@
     hbm = pl.BlockSpec(memory_space=pl.ANY)
     scratch = [
         pltpu.VMEM((8, users, width), BF16),
-        pltpu.VMEM((STAGES, users // 2, width), jnp.int32),
+        pltpu.VMEM((STAGES, users // 4, width), jnp.int32),
         pltpu.VMEM((LAYERS, 8, EMB, width), BF16),
         pltpu.VMEM((LAYERS + 1, 4, EMB, per), BF16),
         pltpu.VMEM((LAYERS, 4, EMB, width), F32),
@@ -404,6 +470,8 @@
         pltpu.VMEM((3, 4, width), F32),
         pltpu.VMEM((4, width), F32),
         pltpu.VMEM((4, width), F32),
+        pltpu.VMEM((4, 1, width), F32),
+        pltpu.VMEM((4, 1, width), F32),
         pltpu.VMEM((8, users), F32),
         pltpu.VMEM((3, 8, users), F32),
         pltpu.VMEM((users, 128), F32),
@@ -419,22 +487,57 @@
     ]
     return pl.pallas_call(
         kernel,
-        out_shape=(jax.ShapeDtypeStruct((EMB, per), BF16),
-                   jax.ShapeDtypeStruct((EMB, width), BF16),
-                   jax.ShapeDtypeStruct((EMB, n_query), BF16)),
+        out_shape=(pltpu.VMEM((EMB, per), BF16),
+                   pltpu.VMEM((EMB, width), BF16),
+                   pltpu.VMEM((EMB, n_query), BF16)),
         in_specs=[hbm, hbm, hbm, hbm],
         out_specs=(vmem, vmem, vmem),
         scratch_shapes=scratch,
         compiler_params=pltpu.CompilerParams(
-            collective_id=0, has_side_effects=True, vmem_limit_bytes=67_000_000),
+            collective_id=0, has_side_effects=True, vmem_limit_bytes=61_600_000),
         name='propagate',
     )(mask_blk, item_shard, user_shard, queries.reshape(1, n_query))
+
+
+def output_kernel(pick_ref, item_ref, user_ref, scores_ref, fi_ref, fu_ref, scores, sem):
+    copies = [pltpu.make_async_copy(item_ref, fi_ref, sem.at[0]),
+              pltpu.make_async_copy(user_ref, fu_ref, sem.at[1])]
+    for copy in copies:
+        copy.start()
+    picked = pick_ref[...].astype(F32).T.astype(BF16)
+    cols = scores.shape[1] // 4
+    for i in range(4):
+        at = pl.ds(i * cols, cols)
+        scores[:, at] = dot(picked, item_ref[:, at], NN)
+        copy = pltpu.make_async_copy(scores.at[:, at], scores_ref.at[:, at], sem.at[2 + i])
+        copy.start()
+        copies.append(copy)
+    for copy in copies:
+        copy.wait()
+
+
+def outputs(fu_t, fi_t, picked_t):
+    n_query = picked_t.shape[1]
+    width, per = fi_t.shape[1], fu_t.shape[1]
+    hbm = pl.BlockSpec(memory_space=pl.ANY)
+    vmem = pl.BlockSpec(memory_space=pltpu.VMEM)
+    args = [pltpu.with_memory_space_constraint(x, pltpu.VMEM) for x in (picked_t, fi_t, fu_t)]
+    return pl.pallas_call(
+        output_kernel,
+        out_shape=(jax.ShapeDtypeStruct((n_query, width), F32),
+                   jax.ShapeDtypeStruct((EMB, width), BF16),
+                   jax.ShapeDtypeStruct((EMB, per), BF16)),
+        in_specs=[vmem, vmem, vmem],
+        out_specs=(hbm, hbm, hbm),
+        scratch_shapes=[pltpu.VMEM((n_query, width), F32), pltpu.SemaphoreType.DMA((6,))],
+        name='outputs',
+    )(*args)
 
 
 def solution(mesh):
     def device_step(mask_blk, user_shard, item_shard, queries):
         fu_t, fi_t, picked_t = propagate(mask_blk, user_shard.T, item_shard.T, queries)
-        scores = dot(picked_t, fi_t, TN)
+        scores, fi_t, fu_t = outputs(fu_t, fi_t, picked_t)
         return fu_t.T, fi_t.T, scores
 
     return jax.shard_map(

time: 108 us -> 98.8 us (0.915)
  Pallas kernels: 104 us -> 97.9 us
  matrix products: 2.79 us -> 0 us
  local copies, waits for them, and re-layouts: 1.32 us -> 0 us
    pallas_call x1 -> x2, Pallas kernels: 104 us -> 97.9 us  [the longest x1 96.2 us: propagate(): pl.pallas_call(kernel, out_shape=(pltpu.VMEM((EMB, per), BF16), pltpu.VME...]
    dot_general x1 -> x0, matrix products: 2.79 us -> none  [dot(): return lax.dot_general(lhs, rhs, dims, preferred_element_type=F32)]
    unnamed x6 -> x0, local copies, waits for them, and re-layouts: 1.32 us -> none
where the time goes in v3:
time: 98.8 us; the launch traced here: 98.7 us
  Pallas kernels  97.9 us (99%)
    pallas_call x1, Pallas kernels, propagate(): pl.pallas_call(kernel, out_shape=(pltpu.VMEM((EMB, per), BF16), pltpu.VME...  96.2 us

profile of v3, /device:TPU:0, one launch (start us, length us, event | category | flops | bytes accessed | tf_op | source)
XLA Modules:
  0.0 98.7 jit_solution(13723673903775399801)
XLA Ops:
  0.6 96.2 %propagate.1 = (bf16[64,128]{1,0:T(8,128)(2,1)S(1)}, bf16[64,2048]{1,0:T(8,128)(2,1)S(1)}, bf16[64,256]{1,0:T(8,128)(2,1)S(1)}) custom-call(s32[512,16384]{1,0:T(8,128)} %mask_ref.1, bf16[64,2048]{1,0:T(8,128)(2,1)} %bitcast.5, bf16[64,128]{1,0:T(8,128)(2,1)} %bitcast.6, s32[1,256]{1,0:T(1,128)} %bitcast.7), custom_call_target="tpu_custom_call" | custom-call | tf_op jit(solution)/shard_map/propagate/pallas_call | solution.py:488
  96.9 1.6 %outputs.1 = (f32[256,2048]{1,0:T(8,128)}, bf16[64,2048]{1,0:T(8,128)(2,1)}, bf16[64,128]{1,0:T(8,128)(2,1)}) custom-call(bf16[64,256]{1,0:T(8,128)(2,1)S(1)} %get-tuple-element.9.pick_ref, bf16[64,2048]{1,0:T(8,128)(2,1)S(1)} %get-tuple-element.10.item_ref, bf16[64,128]{1,0:T(8,128)(2,1)S(1)} %get-tuple-element.11.user_ref), custom_call_target="tpu_custom_call" | custom-call | tf_op jit(solution)/shard_map/outputs/pallas_call | solution.py:525

commit v4 on v3

v4 whole, which is shorter than its diff:
```python
import jax
import jax.numpy as jnp
from jax import lax
from jax.experimental import pallas as pl
from jax.experimental.pallas import tpu as pltpu
from jax.sharding import PartitionSpec as P

LAYERS = 3
EMB = 64
HALF = EMB // 2
QUARTER = EMB // 4
NT = (((1,), (1,)), ((), ()))
NN = (((1,), (0,)), ((), ()))
TN = (((0,), (0,)), ((), ()))
F32 = jnp.float32
BF16 = jnp.bfloat16
STAGES = 8
N_SENT = 24
N_GOT = 61


def dot(lhs, rhs, dims):
    return lax.dot_general(lhs, rhs, dims, preferred_element_type=F32)


def kernel(mask_ref, item_ref, user_ref, query_ref, fu_ref, fi_ref, pick_ref,
           adj, stage, panel, upan, psend, drecv, sacc, hop1, rown, isum, usum,
           colacc, rowacc, deg_send, deg_recv, deg_own, deg_in, deg_fin, deg_oth, far_send, far_in,
           udeg, udeg_in, invu, uacc, upart, uin, pk, qbuf, stage_sem, in_sem, send_sem, recv_sem):
    c = lax.axis_index('col')
    r = lax.axis_index('row')
    users = rowacc.shape[0]
    width = adj.shape[2]
    rows = stage.shape[1]
    per_slot = users // rows
    core, cx, cy = r % 2, (r // 2) % 2, r // 4

    def plane(d, k):
        return ((cy + d // 2) % 2) * 4 + ((cx + d % 2) % 2) * 2 + (core + k) % 2

    def zpeer(k):
        return ((c // 2 + k // 2) % 2) * 2 + (c % 2 + k % 2) % 2

    slots = {d * 2 + k: (c, plane(d, k)) for d in range(4) for k in range(2)}
    partner, xn, yn, dg = slots[1], slots[2], slots[4], slots[6]
    zn = [None] + [(zpeer(k), r) for k in (1, 2, 3)]

    got_index, out_index = {}, {}

    def send(src, dst, device, got, out):
        copy = pltpu.make_async_remote_copy(
            src_ref=src, dst_ref=dst,
            send_sem=send_sem.at[out_index.setdefault(out, len(out_index))],
            recv_sem=recv_sem.at[got_index.setdefault(got, len(got_index))],
            device_id=device, device_id_type=pl.DeviceIdType.MESH)
        copy.start()

    def group(whole, got, out):
        return pltpu.make_async_remote_copy(
            src_ref=whole, dst_ref=whole, send_sem=send_sem.at[out], recv_sem=recv_sem.at[got],
            device_id=partner, device_id_type=pl.DeviceIdType.MESH)

    def arrived(got, whole):
        group(whole, got_index[got], 0).wait_recv()

    def sent(out, whole):
        group(whole, 0, out_index[out]).wait_send()

    def mask_slot(step):
        return (step // per_slot % 4) * 2 + 1 - step // (4 * per_slot)

    def mask_copy(step):
        slot = mask_slot(step)
        part = step % per_slot
        col = plane(slot // 2, slot % 2) * width
        return pltpu.make_async_copy(
            mask_ref.at[pl.ds(pl.multiple_of(part * rows, rows), rows),
                        pl.ds(pl.multiple_of(col, width), width)],
            stage.at[step % STAGES], stage_sem.at[step % STAGES])

    steps = 8 * per_slot
    for s in range(STAGES):
        mask_copy(jnp.int32(s)).start()

    inputs = [pltpu.make_async_copy(item_ref, panel.at[0, 0], in_sem.at[0]),
              pltpu.make_async_copy(user_ref, upan.at[0, c], in_sem.at[1]),
              pltpu.make_async_copy(query_ref, qbuf, in_sem.at[2])]
    for copy in inputs:
        copy.start()

    barrier = pltpu.get_barrier_semaphore()
    peers = tuple(slots[k] for k in range(1, 8)) + (zn[1], zn[2], zn[3])
    for device in peers:
        pl.semaphore_signal(barrier, inc=1, device_id=device, device_id_type=pl.DeviceIdType.MESH)

    rowacc[...] = jnp.zeros_like(rowacc)
    colacc[...] = jnp.zeros_like(colacc)

    def piece(h, i):
        return pl.ds(h * HALF + i * QUARTER, QUARTER)

    def gather_start(n, i):
        own = panel.at[n, 0]
        for h in (0, 1):
            got = ('forward', n, i) if h == 0 else ('near', n)
            at, to = piece(h, i), piece(1 - h, i)
            send(own.at[at], panel.at[n, 2, at], xn, got, ('gather', n))
            send(own.at[to], panel.at[n, 4, to], yn, got, ('gather', n))
        if i:
            send(own, panel.at[n, 1], partner, ('p0', n), ('gather', n))

    def gather_forward(n, i):
        arrived(('forward', n, i), panel.at[n, 2, pl.ds(0, HALF)])
        at, to = piece(0, i), piece(1, i)
        send(panel.at[n, 2, at], panel.at[n, 6, at], yn, ('last', n), ('gather', n))
        send(panel.at[n, 4, to], panel.at[n, 6, to], xn, ('last', n), ('gather', n))

    def gather_near(n):
        arrived(('near', n), panel.at[n, 2])
        send(panel.at[n, 2], panel.at[n, 3], partner, ('p12', n), ('gather', n))
        send(panel.at[n, 4], panel.at[n, 5], partner, ('p12', n), ('gather', n))

    def gather_last(n):
        arrived(('last', n), panel.at[n, 6])
        send(panel.at[n, 6], panel.at[n, 7], partner, ('p3', n), ('gather', n))

    def zgather_start(n):
        for k in (3, 2, 1):
            send(upan.at[n, c], upan.at[n, c], zn[k], ('zgather', n), ('zgather', n))

    def zgather_wait(n):
        arrived(('zgather', n), upan.at[n, pl.ds(0, 3)])
        return jnp.concatenate([upan[n, k] for k in range(4)], axis=1)

    def zsum_start(n, acc):
        acc_t = acc.T
        for k in range(4):
            upart[n, k] = acc_t[:, k * 128:(k + 1) * 128]
        for k in (3, 2, 1):
            send(upart.at[n, zpeer(k)], uin.at[n, k - 1], zn[k], ('zsum', n), ('zsum', n))

    def zsum_wait(n):
        arrived(('zsum', n), uin.at[n])
        total = (upart[n, c] + uin[n, 0]) + (uin[n, 1] + uin[n, 2])
        nxt = total.astype(BF16)
        usum[...] = usum[...] + nxt.astype(F32)
        return nxt

    def mask_step(step, carry):
        mask_copy(step).wait()
        slot = mask_slot(step)
        part = step % per_slot
        buf = step % STAGES

        def convert(i, col):
            at = pl.multiple_of(i * 16, 16)
            x = stage[buf, pl.ds(at, 16), :].astype(F32)
            row = pl.multiple_of(part * rows + i * 16, 16)
            adj[slot, pl.ds(row, 16), :] = x.astype(BF16)
            lanes = x[:, :128]
            for t in range(1, width // 128):
                lanes = lanes + x[:, t * 128:(t + 1) * 128]
            rowacc[pl.ds(row, 16), :] += lanes
            return col + (x[:8] + x[8:])

        colacc[slot] += lax.fori_loop(0, rows // 16, convert, jnp.zeros((8, width), F32), unroll=2)

        @pl.when(step + STAGES < steps)
        def _():
            mask_copy(step + STAGES).start()

        return carry

    with jax.named_scope('mask_a'):
        lax.fori_loop(0, steps // 4, mask_step, 0)
    with jax.named_scope('barrier'):
        pl.semaphore_wait(barrier, len(peers))
    with jax.named_scope('inputs'):
        for copy in inputs:
            copy.wait()
        gather_start(0, 0)
        gather_start(0, 1)
        zgather_start(0)
        isum[...] = panel[0, 0].astype(F32)
        usum[...] = upan[0, c].astype(F32)
    with jax.named_scope('mask_b'):
        lax.fori_loop(steps // 4, steps * 5 // 8, mask_step, 0)
        for d in range(4):
            deg_send[d:d + 1, :] = jnp.sum(colacc[2 * d + 1], axis=0, keepdims=True)
        send(deg_send, deg_recv, partner, 'dp', 'dp')
    with jax.named_scope('mask_c'):
        lax.fori_loop(steps * 5 // 8, steps, mask_step, 0)

    with jax.named_scope('deg_sum'):
        udeg[...] = dot(jnp.ones((8, 128), BF16), rowacc[...].astype(BF16), NT)
        for k in (3, 2, 1):
            send(udeg, udeg_in.at[k - 1], zn[k], 'zd', 'zd')
        mine = jnp.concatenate(
            [jnp.sum(colacc[2 * d], axis=0, keepdims=True) for d in range(4)], axis=0)
    with jax.named_scope('deg_partner'):
        arrived('dp', deg_recv)
        deg_own[...] = mine + deg_recv[...]
        for k, device in enumerate((xn, yn, dg)):
            send(deg_own, deg_in.at[k], device, 'ds', 'ds')
        for d in range(4):
            far_send[d] = deg_own[d:d + 1, :]
            send(far_send.at[d], far_in.at[d], slots[2 * (3 - d) + 1], 'far', 'far')
    with jax.named_scope('deg_users'):
        arrived('zd', udeg_in)
        du = (udeg[...] + udeg_in[0]) + (udeg_in[1] + udeg_in[2])
        inv = lax.rsqrt(jnp.maximum(du, 1.0))
        invu[...] = jnp.broadcast_to(inv[0:1, :], (128, users)).T
    with jax.named_scope('deg_items'):
        arrived('ds', deg_in)
    with jax.named_scope('deg_inv'):
        for d in range(4):
            total = ((deg_own[d:d + 1, :] + deg_in[0, (d ^ 1):(d ^ 1) + 1, :])
                     + (deg_in[1, (d ^ 2):(d ^ 2) + 1, :] + deg_in[2, (d ^ 3):(d ^ 3) + 1, :]))
            deg_fin[d:d + 1, :] = lax.rsqrt(jnp.maximum(total, 1.0))
        send(deg_fin, deg_oth, partner, 'df', 'df')
        arrived('far', far_in)
        for i in (0, 1):
            gather_forward(0, i)
        gather_near(0)

    def normalize(slot, at=0, size=width):
        d = slot // 2
        cols = pl.ds(at, size)
        if slot == 7:
            total = (far_in[3, :, cols] + far_in[2, :, cols]) + (far_in[1, :, cols] + far_in[0, :, cols])
            inv_item = lax.rsqrt(jnp.maximum(total, 1.0))
        else:
            inv_item = (deg_oth if slot % 2 else deg_fin)[d:d + 1, cols]

        def scale(i, carry):
            row = pl.ds(pl.multiple_of(i * 16, 16), 16)
            inv_user = jnp.concatenate([invu[row, :]] * (size // 128), axis=1)
            adj[slot, row, cols] = adj[slot, row, cols] * (inv_user * inv_item).astype(BF16)
            return carry

        lax.fori_loop(0, users // 16, scale, 0, unroll=2)

    starts = (0, width // 4)
    sizes = (width // 4, width - width // 4)
    splits = [pl.ds(at, size) for at, size in zip(starts, sizes)]
    lo, hi = pl.ds(0, HALF), pl.ds(HALF, HALF)

    def items_diagonal(n, i):
        cols = splits[i]
        send(sacc.at[n, 3, lo, cols], hop1.at[n, 0, :, cols], xn, ('hop1', n), ('sum', n))
        send(sacc.at[n, 3, hi, cols], hop1.at[n, 1, :, cols], yn, ('hop1', n), ('sum', n))

    def items_x(n):
        send(sacc.at[n, 1, lo], rown.at[n, 0], xn, ('direct', n), ('sum', n))

    def items_y(n):
        send(sacc.at[n, 2, hi], rown.at[n, 3], yn, ('direct', n), ('sum', n))

    def away(n, u, d):
        psend[n, d] = dot(u, adj[2 * d + 1], NN)
        send(psend.at[n, d], drecv.at[n, d], partner, ('partner', n, d), ('items', n))

    def near(n, u, d):
        part = dot(u, adj[2 * d], NN)
        if d:
            arrived(('partner', n, d), drecv.at[n, d])
            part = part + drecv[n, d]
        sacc[n, d] = part

    def items_first(u):
        for i, cols in enumerate(splits):
            normalize(7, starts[i], sizes[i])
            psend[0, 3, :, cols] = dot(u, adj[7, :, cols], NN)
            send(psend.at[0, 3, :, cols], drecv.at[0, 3, :, cols], partner, ('partner', 0, 3, i), ('items', 0))
        for i, cols in enumerate(splits):
            normalize(6, starts[i], sizes[i])
            own = dot(u, adj[6, :, cols], NN)
            arrived(('partner', 0, 3, i), drecv.at[0, 3, :, cols])
            sacc[0, 3, :, cols] = own + drecv[0, 3, :, cols]
            items_diagonal(0, i)
        arrived('df', deg_oth)

        def both(slot, step, d):
            normalize(slot)
            step(0, u, d)

        both(3, away, 1)
        both(5, away, 2)
        both(2, near, 1)
        items_x(0)
        both(1, away, 0)
        both(4, near, 2)
        items_y(0)
        both(0, near, 0)

    def items_later(n, u, hooks):
        away(n, u, 3)
        away(n, u, 1)
        hooks[0]()
        near(n, u, 3)
        hooks[1]()
        away(n, u, 2)
        away(n, u, 0)
        near(n, u, 1)
        hooks[2]()
        near(n, u, 2)
        near(n, u, 0)

    def items_mid(n, i):
        if i == 0:
            arrived(('hop1', n), hop1.at[n])
        at = pl.ds(i * QUARTER, QUARTER)
        sacc[n, 2, piece(0, i)] = sacc[n, 2, piece(0, i)] + hop1[n, 0, at]
        send(sacc.at[n, 2, piece(0, i)], rown.at[n, 2, at], yn, ('hop2', n, i), ('sum', n))
        sacc[n, 1, piece(1, i)] = sacc[n, 1, piece(1, i)] + hop1[n, 1, at]
        send(sacc.at[n, 1, piece(1, i)], rown.at[n, 1, at], xn, ('hop2', n, i), ('sum', n))

    def items_finish(n, i):
        if i == 0:
            arrived(('partner', n, 0), drecv.at[n, 0])
            arrived(('direct', n), rown.at[n, pl.ds(0, 2)])
        arrived(('hop2', n, i), rown.at[n, 0])
        at = pl.ds(i * QUARTER, QUARTER)
        for h in (0, 1):
            rows_h = piece(h, i)
            total = ((sacc[n, 0, rows_h] + drecv[n, 0, rows_h]) + rown[n, h, at]) + rown[n, 2 + h, at]
            nxt = total.astype(BF16)
            isum[rows_h] = isum[rows_h] + nxt.astype(F32)
            if n + 1 < LAYERS:
                panel[n + 1, 0, rows_h] = nxt

    def user_partial(n, near_done=False, hook=None):
        def some(first, stride, count):
            def one(j, carry):
                at = first + stride * j
                uacc[...] += dot(adj[at], panel[n, at], NT)
                return carry

            lax.fori_loop(0, count, one, 0)

        arrived(('p0', n), panel.at[n, 1])
        uacc[...] = dot(adj[0], panel[n, 0], NT)
        some(1, 1, 1)
        if not near_done:
            gather_near(n)
        some(2, 2, 2)
        arrived(('p12', n), panel.at[n, pl.ds(2, 2)])
        some(3, 2, 2)
        if hook is not None:
            hook()
        gather_last(n)
        some(6, 1, 1)
        arrived(('p3', n), panel.at[n, 7])
        some(7, 1, 1)
        return uacc[...]

    scope = jax.named_scope

    def mid(n):
        items_mid(n, 0)
        items_mid(n, 1)

    def finish(n, i):
        with scope(f'finish{n}{i}'):
            items_finish(n, i)
            gather_start(n + 1, i)

    def forward(n, i):
        with scope(f'forward{n}{i}'):
            gather_forward(n, i)

    def launch1():
        forward(1, 1)
        items_diagonal(1, 0)
        items_diagonal(1, 1)

    def nothing():
        pass

    pick_all = pk.at[pl.ds(3, 3), lo]
    with scope('u0'):
        u0 = zgather_wait(0)
    with scope('items0'):
        items_first(u0)
    with scope('user0'):
        zsum_start(0, user_partial(0, near_done=True, hook=lambda: mid(0)))
    finish(0, 0)
    with scope('zsum0'):
        upan[1, c] = zsum_wait(0)
        zgather_start(1)
    finish(0, 1)
    with scope('zgather1'):
        u1 = zgather_wait(1)
    with scope('items1'):
        forward(1, 0)
        items_later(1, u1, (nothing, launch1, nothing))
        items_x(1)
        items_y(1)
    with scope('user1'):
        zsum_start(1, user_partial(1))
    with scope('mid1'):
        mid(1)
    with scope('zsum1'):
        upan[2, c] = zsum_wait(1)
        zgather_start(2)
    with scope('zgather2'):
        u2 = zgather_wait(2)
    with scope('items2'):
        items_later(2, u2, (lambda: finish(1, 0), lambda: finish(1, 1), lambda: forward(2, 0)))
        forward(2, 1)
        items_diagonal(2, 0)
        items_diagonal(2, 1)
        items_x(2)
        items_y(2)
    with scope('user2'):
        zsum_start(2, user_partial(2))
    with scope('mid2'):
        items_mid(2, 0)
    with scope('zsum2'):
        zsum_wait(2)
        final_user = (usum[...] / (LAYERS + 1)).astype(BF16)
        fu_ref[...] = final_user
        upan[3, c] = final_user
        zgather_start(3)
    with scope('zgather3'):
        ufin = zgather_wait(3)
    with scope('pick'):
        local = qbuf[...] - r * users
        chosen = (lax.broadcasted_iota(jnp.int32, (users, local.shape[1]), 0)
                  == jnp.broadcast_to(local, (users, local.shape[1]))).astype(F32).astype(BF16)
        pk[0] = dot(ufin, chosen, NN).astype(BF16)
        send(pk.at[0], pk.at[1], partner, 'pick', 'pick')
        arrived('pick', pk.at[1])
        pk[2] = pk[0] + pk[1]
        mine = pl.ds(pl.multiple_of(core * HALF, HALF), HALF)
        for k, device in enumerate((xn, yn, dg)):
            send(pk.at[2, mine], pk.at[3 + k, mine], device, 'picks', 'picks')
        items_mid(2, 1)
    with scope('finish20'):
        items_finish(2, 0)
    with scope('picked'):
        arrived('picks', pick_all)
        pk[6, mine] = (pk[2, mine] + pk[3, mine]) + (pk[4, mine] + pk[5, mine])
        send(pk.at[6, mine], pk.at[6, mine], partner, 'picked', 'picked')
    with scope('finish21'):
        items_finish(2, 1)
        fi_ref[...] = (isum[...] / (LAYERS + 1)).astype(BF16)
    with scope('pick_half'):
        arrived('picked', pk.at[6, lo])
        pick_ref[...] = pk[6]
    with scope('drain'):
        for n in range(LAYERS):
            sent(('gather', n), panel.at[n, pl.ds(0, 7)])
            sent(('items', n), psend.at[n])
            sent(('sum', n), sacc.at[n, pl.ds(1, 3)])
            sent(('zsum', n), uin.at[n])
        for n in range(LAYERS + 1):
            sent(('zgather', n), upan.at[n, pl.ds(0, 3)])
        for out, whole in (('dp', deg_send), ('zd', udeg_in), ('ds', deg_in), ('far', far_in),
                           ('df', deg_fin), ('pick', pk.at[0]), ('picks', pick_all), ('picked', pk.at[6, lo])):
            sent(out, whole)


def propagate(mask_blk, user_shard, item_shard, queries):
    users, items = mask_blk.shape
    width = items // 8
    per = user_shard.shape[1]
    n_query = queries.shape[0]
    vmem = pl.BlockSpec(memory_space=pltpu.VMEM)
    hbm = pl.BlockSpec(memory_space=pl.ANY)
    scratch = [
        pltpu.VMEM((8, users, width), BF16),
        pltpu.VMEM((STAGES, users // 4, width), jnp.int32),
        pltpu.VMEM((LAYERS, 8, EMB, width), BF16),
        pltpu.VMEM((LAYERS + 1, 4, EMB, per), BF16),
        pltpu.VMEM((LAYERS, 4, EMB, width), F32),
        pltpu.VMEM((LAYERS, 4, EMB, width), F32),
        pltpu.VMEM((LAYERS, 4, EMB, width), F32),
        pltpu.VMEM((LAYERS, 2, HALF, width), F32),
        pltpu.VMEM((LAYERS, 4, HALF, width), F32),
        pltpu.VMEM((EMB, width), F32),
        pltpu.VMEM((EMB, per), F32),
        pltpu.VMEM((8, 8, width), F32),
        pltpu.VMEM((users, 128), F32),
        pltpu.VMEM((4, width), F32),
        pltpu.VMEM((4, width), F32),
        pltpu.VMEM((4, width), F32),
        pltpu.VMEM((3, 4, width), F32),
        pltpu.VMEM((4, width), F32),
        pltpu.VMEM((4, width), F32),
        pltpu.VMEM((4, 1, width), F32),
        pltpu.VMEM((4, 1, width), F32),
        pltpu.VMEM((8, users), F32),
        pltpu.VMEM((3, 8, users), F32),
        pltpu.VMEM((users, 128), F32),
        pltpu.VMEM((users, EMB), F32),
        pltpu.VMEM((LAYERS, 4, EMB, per), F32),
        pltpu.VMEM((LAYERS, 3, EMB, per), F32),
        pltpu.VMEM((7, EMB, n_query), BF16),
        pltpu.VMEM((1, n_query), jnp.int32),
        pltpu.SemaphoreType.DMA((STAGES,)),
        pltpu.SemaphoreType.DMA((3,)),
        pltpu.SemaphoreType.DMA((N_SENT,)),
        pltpu.SemaphoreType.DMA((N_GOT,)),
    ]
    return pl.pallas_call(
        kernel,
        out_shape=(pltpu.VMEM((EMB, per), BF16),
                   pltpu.VMEM((EMB, width), BF16),
                   pltpu.VMEM((EMB, n_query), BF16)),
        in_specs=[hbm, hbm, hbm, hbm],
        out_specs=(vmem, vmem, vmem),
        scratch_shapes=scratch,
        compiler_params=pltpu.CompilerParams(
            collective_id=0, has_side_effects=True, vmem_limit_bytes=61_600_000),
        name='propagate',
    )(mask_blk, item_shard, user_shard, queries.reshape(1, n_query))


def output_kernel(pick_ref, item_ref, user_ref, scores_ref, fi_ref, fu_ref, scores, sem):
    copies = [pltpu.make_async_copy(item_ref, fi_ref, sem.at[0]),
              pltpu.make_async_copy(user_ref, fu_ref, sem.at[1])]
    for copy in copies:
        copy.start()
    picked = pick_ref[...].astype(F32).T.astype(BF16)
    cols = scores.shape[1] // 4
    for i in range(4):
        at = pl.ds(i * cols, cols)
        scores[:, at] = dot(picked, item_ref[:, at], NN)
        copy = pltpu.make_async_copy(scores.at[:, at], scores_ref.at[:, at], sem.at[2 + i])
        copy.start()
        copies.append(copy)
    for copy in copies:
        copy.wait()


def outputs(fu_t, fi_t, picked_t):
    n_query = picked_t.shape[1]
    width, per = fi_t.shape[1], fu_t.shape[1]
    hbm = pl.BlockSpec(memory_space=pl.ANY)
    vmem = pl.BlockSpec(memory_space=pltpu.VMEM)
    args = [pltpu.with_memory_space_constraint(x, pltpu.VMEM) for x in (picked_t, fi_t, fu_t)]
    return pl.pallas_call(
        output_kernel,
        out_shape=(jax.ShapeDtypeStruct((n_query, width), F32),
                   jax.ShapeDtypeStruct((EMB, width), BF16),
                   jax.ShapeDtypeStruct((EMB, per), BF16)),
        in_specs=[vmem, vmem, vmem],
        out_specs=(hbm, hbm, hbm),
        scratch_shapes=[pltpu.VMEM((n_query, width), F32), pltpu.SemaphoreType.DMA((6,))],
        name='outputs',
    )(*args)


def solution(mesh):
    def device_step(mask_blk, user_shard, item_shard, queries):
        fu_t, fi_t, picked_t = propagate(mask_blk, user_shard.T, item_shard.T, queries)
        scores, fi_t, fu_t = outputs(fu_t, fi_t, picked_t)
        return fu_t.T, fi_t.T, scores

    return jax.shard_map(
        device_step, mesh=mesh,
        in_specs=(P('row', 'col'), P(('row', 'col'), None), P(('col', 'row'), None), P()),
        out_specs=(P(('row', 'col'), None), P(('col', 'row'), None), P(None, ('col', 'row'))),
        check_vma=False)
```

time: 98.8 us -> 94.6 us (0.957)
  Pallas kernels: 97.9 us -> 93.7 us
    pallas_call x1, Pallas kernels: 96.2 us -> 92 us  [propagate(): pl.pallas_call(kernel, out_shape=(pltpu.VMEM((EMB, per), BF16), pltpu.VME...]
where the time goes in v4:
time: 94.6 us; the launch traced here: 94.5 us
  Pallas kernels  93.7 us (99%)
    pallas_call x1, Pallas kernels, propagate(): pl.pallas_call(kernel, out_shape=(pltpu.VMEM((EMB, per), BF16), pltpu.VME...  92 us

profile of v4, /device:TPU:0, one launch (start us, length us, event | category | flops | bytes accessed | tf_op | source)
XLA Modules:
  0.0 94.5 jit_solution(12795857336168336774)
XLA Ops:
  0.6 92.0 %propagate.1 = (bf16[64,128]{1,0:T(8,128)(2,1)S(1)}, bf16[64,2048]{1,0:T(8,128)(2,1)S(1)}, bf16[64,256]{1,0:T(8,128)(2,1)S(1)}) custom-call(s32[512,16384]{1,0:T(8,128)} %mask_ref.1, bf16[64,2048]{1,0:T(8,128)(2,1)} %bitcast.5, bf16[64,128]{1,0:T(8,128)(2,1)} %bitcast.6, s32[1,256]{1,0:T(1,128)} %bitcast.7), custom_call_target="tpu_custom_call" | custom-call | tf_op jit(solution)/shard_map/propagate/pallas_call | solution.py:506
  92.7 1.6 %outputs.1 = (f32[256,2048]{1,0:T(8,128)}, bf16[64,2048]{1,0:T(8,128)(2,1)}, bf16[64,128]{1,0:T(8,128)(2,1)}) custom-call(bf16[64,256]{1,0:T(8,128)(2,1)S(1)} %get-tuple-element.9.pick_ref, bf16[64,2048]{1,0:T(8,128)(2,1)S(1)} %get-tuple-element.10.item_ref, bf16[64,128]{1,0:T(8,128)(2,1)S(1)} %get-tuple-element.11.user_ref), custom_call_target="tpu_custom_call" | custom-call | tf_op jit(solution)/shard_map/outputs/pallas_call | solution.py:543

commit v5 on v4

--- a/solution.py
+++ b/solution.py
@@ -15,8 +15,8 @@
 F32 = jnp.float32
 BF16 = jnp.bfloat16
 STAGES = 8
-N_SENT = 24
-N_GOT = 61
+N_SENT = 13
+N_GOT = 43
 
 
 def dot(lhs, rhs, dims):
@@ -47,11 +47,14 @@
 
     got_index, out_index = {}, {}
 
+    def parity(key):
+        return key if isinstance(key, str) else (key[0], key[1] % 2) + key[2:]
+
     def send(src, dst, device, got, out):
         copy = pltpu.make_async_remote_copy(
             src_ref=src, dst_ref=dst,
             send_sem=send_sem.at[out_index.setdefault(out, len(out_index))],
-            recv_sem=recv_sem.at[got_index.setdefault(got, len(got_index))],
+            recv_sem=recv_sem.at[got_index.setdefault(parity(got), len(got_index))],
             device_id=device, device_id_type=pl.DeviceIdType.MESH)
         copy.start()
 
@@ -61,7 +64,7 @@
             device_id=partner, device_id_type=pl.DeviceIdType.MESH)
 
     def arrived(got, whole):
-        group(whole, got_index[got], 0).wait_recv()
+        group(whole, got_index[parity(got)], 0).wait_recv()
 
     def sent(out, whole):
         group(whole, 0, out_index[out]).wait_send()
@@ -104,32 +107,32 @@
         for h in (0, 1):
             got = ('forward', n, i) if h == 0 else ('near', n)
             at, to = piece(h, i), piece(1 - h, i)
-            send(own.at[at], panel.at[n, 2, at], xn, got, ('gather', n))
-            send(own.at[to], panel.at[n, 4, to], yn, got, ('gather', n))
+            send(own.at[at], panel.at[n, 2, at], xn, got, 'gather')
+            send(own.at[to], panel.at[n, 4, to], yn, got, 'gather')
         if i:
-            send(own, panel.at[n, 1], partner, ('p0', n), ('gather', n))
+            send(own, panel.at[n, 1], partner, ('p0', n), 'gather')
 
     def gather_forward(n, i):
         arrived(('forward', n, i), panel.at[n, 2, pl.ds(0, HALF)])
         at, to = piece(0, i), piece(1, i)
-        send(panel.at[n, 2, at], panel.at[n, 6, at], yn, ('last', n), ('gather', n))
-        send(panel.at[n, 4, to], panel.at[n, 6, to], xn, ('last', n), ('gather', n))
+        send(panel.at[n, 2, at], panel.at[n, 6, at], yn, ('last', n), 'gather')
+        send(panel.at[n, 4, to], panel.at[n, 6, to], xn, ('last', n), 'gather')
 
     def gather_near(n):
         arrived(('near', n), panel.at[n, 2])
-        send(panel.at[n, 2], panel.at[n, 3], partner, ('p12', n), ('gather', n))
-        send(panel.at[n, 4], panel.at[n, 5], partner, ('p12', n), ('gather', n))
+        send(panel.at[n, 2], panel.at[n, 3], partner, ('p12', n), 'gather')
+        send(panel.at[n, 4], panel.at[n, 5], partner, ('p12', n), 'gather')
 
     def gather_last(n):
         arrived(('last', n), panel.at[n, 6])
-        send(panel.at[n, 6], panel.at[n, 7], partner, ('p3', n), ('gather', n))
+        send(panel.at[n, 6], panel.at[n, 7], partner, ('p3', n), 'gather')
 
     def zgather_start(n):
         for k in (3, 2, 1):
-            send(upan.at[n, c], upan.at[n, c], zn[k], ('zgather', n), ('zgather', n))
+            send(upan.at[n, c], upan.at[n, c], zn[k], 'zgather', 'zgather')
 
     def zgather_wait(n):
-        arrived(('zgather', n), upan.at[n, pl.ds(0, 3)])
+        arrived('zgather', upan.at[n, pl.ds(0, 3)])
         return jnp.concatenate([upan[n, k] for k in range(4)], axis=1)
 
     def zsum_start(n, acc):
@@ -137,10 +140,10 @@
         for k in range(4):
             upart[n, k] = acc_t[:, k * 128:(k + 1) * 128]
         for k in (3, 2, 1):
-            send(upart.at[n, zpeer(k)], uin.at[n, k - 1], zn[k], ('zsum', n), ('zsum', n))
+            send(upart.at[n, zpeer(k)], uin.at[n, k - 1], zn[k], 'zsum', 'zsum')
 
     def zsum_wait(n):
-        arrived(('zsum', n), uin.at[n])
+        arrived('zsum', uin.at[n])
         total = (upart[n, c] + uin[n, 0]) + (uin[n, 1] + uin[n, 2])
         nxt = total.astype(BF16)
         usum[...] = usum[...] + nxt.astype(F32)
@@ -232,33 +235,36 @@
         else:
             inv_item = (deg_oth if slot % 2 else deg_fin)[d:d + 1, cols]
 
+        step = 16 * max(1, width // 2 // size)
+
         def scale(i, carry):
-            row = pl.ds(pl.multiple_of(i * 16, 16), 16)
-            inv_user = jnp.concatenate([invu[row, :]] * (size // 128), axis=1)
-            adj[slot, row, cols] = adj[slot, row, cols] * (inv_user * inv_item).astype(BF16)
+            for j in range(step // 16):
+                row = pl.ds(pl.multiple_of(i * step + j * 16, 16), 16)
+                inv_user = jnp.concatenate([invu[row, :]] * (size // 128), axis=1)
+                adj[slot, row, cols] = adj[slot, row, cols] * (inv_user * inv_item).astype(BF16)
             return carry
 
-        lax.fori_loop(0, users // 16, scale, 0, unroll=2)
-
-    starts = (0, width // 4)
-    sizes = (width // 4, width - width // 4)
+        lax.fori_loop(0, users // step, scale, 0, unroll=2)
+
+    sizes = (width // 8, width // 4, width - 3 * width // 8)
+    starts = (0, width // 8, 3 * width // 8)
     splits = [pl.ds(at, size) for at, size in zip(starts, sizes)]
     lo, hi = pl.ds(0, HALF), pl.ds(HALF, HALF)
 
-    def items_diagonal(n, i):
-        cols = splits[i]
-        send(sacc.at[n, 3, lo, cols], hop1.at[n, 0, :, cols], xn, ('hop1', n), ('sum', n))
-        send(sacc.at[n, 3, hi, cols], hop1.at[n, 1, :, cols], yn, ('hop1', n), ('sum', n))
+    def items_diagonal(n, i=None):
+        cols = pl.ds(0, width) if i is None else splits[i]
+        send(sacc.at[n, 3, lo, cols], hop1.at[n, 0, :, cols], xn, ('hop1', n), 'sum')
+        send(sacc.at[n, 3, hi, cols], hop1.at[n, 1, :, cols], yn, ('hop1', n), 'sum')
 
     def items_x(n):
-        send(sacc.at[n, 1, lo], rown.at[n, 0], xn, ('direct', n), ('sum', n))
+        send(sacc.at[n, 1, lo], rown.at[n, 0], xn, ('direct', n), 'sum')
 
     def items_y(n):
-        send(sacc.at[n, 2, hi], rown.at[n, 3], yn, ('direct', n), ('sum', n))
+        send(sacc.at[n, 2, hi], rown.at[n, 3], yn, ('direct', n), 'sum')
 
     def away(n, u, d):
         psend[n, d] = dot(u, adj[2 * d + 1], NN)
-        send(psend.at[n, d], drecv.at[n, d], partner, ('partner', n, d), ('items', n))
+        send(psend.at[n, d], drecv.at[n, d], partner, ('partner', n, d), 'items')
 
     def near(n, u, d):
         part = dot(u, adj[2 * d], NN)
@@ -268,30 +274,49 @@
         sacc[n, d] = part
 
     def items_first(u):
-        for i, cols in enumerate(splits):
+        def theirs(i):
+            cols = splits[i]
             normalize(7, starts[i], sizes[i])
             psend[0, 3, :, cols] = dot(u, adj[7, :, cols], NN)
-            send(psend.at[0, 3, :, cols], drecv.at[0, 3, :, cols], partner, ('partner', 0, 3, i), ('items', 0))
-        for i, cols in enumerate(splits):
+            send(psend.at[0, 3, :, cols], drecv.at[0, 3, :, cols], partner, ('partner', 0, 3, i), 'items')
+
+        def ours(i):
+            cols = splits[i]
             normalize(6, starts[i], sizes[i])
-            own = dot(u, adj[6, :, cols], NN)
-            arrived(('partner', 0, 3, i), drecv.at[0, 3, :, cols])
-            sacc[0, 3, :, cols] = own + drecv[0, 3, :, cols]
+            sacc[0, 3, :, cols] = dot(u, adj[6, :, cols], NN)
+
+        def both(i):
+            cols = splits[i]
+            with jax.named_scope(f'w6{i}'):
+                arrived(('partner', 0, 3, i), drecv.at[0, 3, :, cols])
+                sacc[0, 3, :, cols] = sacc[0, 3, :, cols] + drecv[0, 3, :, cols]
             items_diagonal(0, i)
+
+        theirs(0)
+        ours(0)
+        theirs(1)
+        theirs(2)
+        both(0)
+        ours(1)
+        both(1)
+        ours(2)
+        both(2)
         arrived('df', deg_oth)
 
-        def both(slot, step, d):
-            normalize(slot)
-            step(0, u, d)
-
-        both(3, away, 1)
-        both(5, away, 2)
-        both(2, near, 1)
+        normalize(3)
+        away(0, u, 1)
+        normalize(5)
+        away(0, u, 2)
+        normalize(2)
+        near(0, u, 1)
         items_x(0)
-        both(1, away, 0)
-        both(4, near, 2)
+        normalize(1)
+        away(0, u, 0)
+        normalize(4)
+        near(0, u, 2)
         items_y(0)
-        both(0, near, 0)
+        normalize(0)
+        near(0, u, 0)
 
     def items_later(n, u, hooks):
         away(n, u, 3)
@@ -311,9 +336,9 @@
             arrived(('hop1', n), hop1.at[n])
         at = pl.ds(i * QUARTER, QUARTER)
         sacc[n, 2, piece(0, i)] = sacc[n, 2, piece(0, i)] + hop1[n, 0, at]
-        send(sacc.at[n, 2, piece(0, i)], rown.at[n, 2, at], yn, ('hop2', n, i), ('sum', n))
+        send(sacc.at[n, 2, piece(0, i)], rown.at[n, 2, at], yn, ('hop2', n, i), 'sum')
         sacc[n, 1, piece(1, i)] = sacc[n, 1, piece(1, i)] + hop1[n, 1, at]
-        send(sacc.at[n, 1, piece(1, i)], rown.at[n, 1, at], xn, ('hop2', n, i), ('sum', n))
+        send(sacc.at[n, 1, piece(1, i)], rown.at[n, 1, at], xn, ('hop2', n, i), 'sum')
 
     def items_finish(n, i):
         if i == 0:
@@ -371,13 +396,11 @@
 
     def launch1():
         forward(1, 1)
-        items_diagonal(1, 0)
-        items_diagonal(1, 1)
+        items_diagonal(1)
 
     def nothing():
         pass
 
-    pick_all = pk.at[pl.ds(3, 3), lo]
     with scope('u0'):
         u0 = zgather_wait(0)
     with scope('items0'):
@@ -408,14 +431,18 @@
     with scope('items2'):
         items_later(2, u2, (lambda: finish(1, 0), lambda: finish(1, 1), lambda: forward(2, 0)))
         forward(2, 1)
-        items_diagonal(2, 0)
-        items_diagonal(2, 1)
+        items_diagonal(2)
         items_x(2)
         items_y(2)
     with scope('user2'):
         zsum_start(2, user_partial(2))
     with scope('mid2'):
         items_mid(2, 0)
+
+        @pl.when(core == 0)
+        def _():
+            items_mid(2, 1)
+
     with scope('zsum2'):
         zsum_wait(2)
         final_user = (usum[...] / (LAYERS + 1)).astype(BF16)
@@ -429,35 +456,47 @@
         chosen = (lax.broadcasted_iota(jnp.int32, (users, local.shape[1]), 0)
                   == jnp.broadcast_to(local, (users, local.shape[1]))).astype(F32).astype(BF16)
         pk[0] = dot(ufin, chosen, NN).astype(BF16)
-        send(pk.at[0], pk.at[1], partner, 'pick', 'pick')
-        arrived('pick', pk.at[1])
-        pk[2] = pk[0] + pk[1]
-        mine = pl.ds(pl.multiple_of(core * HALF, HALF), HALF)
-        for k, device in enumerate((xn, yn, dg)):
-            send(pk.at[2, mine], pk.at[3 + k, mine], device, 'picks', 'picks')
-        items_mid(2, 1)
+
+        @pl.when(core == 0)
+        def _():
+            send(pk.at[0], pk.at[1], partner, 'pick', 'pick')
+
+        @pl.when(core == 1)
+        def _():
+            arrived('pick', pk.at[1])
+            pk[2] = pk[0] + pk[1]
+            for k, device in enumerate((xn, yn, dg)):
+                send(pk.at[2], pk.at[3 + k], device, 'picks', 'picks')
+            items_mid(2, 1)
+
     with scope('finish20'):
         items_finish(2, 0)
     with scope('picked'):
-        arrived('picks', pick_all)
-        pk[6, mine] = (pk[2, mine] + pk[3, mine]) + (pk[4, mine] + pk[5, mine])
-        send(pk.at[6, mine], pk.at[6, mine], partner, 'picked', 'picked')
+        @pl.when(core == 1)
+        def _():
+            arrived('picks', pk.at[pl.ds(3, 3)])
+            pk[6] = (pk[2] + pk[3]) + (pk[4] + pk[5])
+            send(pk.at[6], pk.at[6], partner, 'picked', 'picked')
+            sent('picks', pk.at[pl.ds(3, 3)])
+            sent('picked', pk.at[6])
+
+        @pl.when(core == 0)
+        def _():
+            arrived('picked', pk.at[6])
+            sent('pick', pk.at[0])
+
+        pick_ref[...] = pk[6].astype(F32).T.astype(BF16)
     with scope('finish21'):
         items_finish(2, 1)
         fi_ref[...] = (isum[...] / (LAYERS + 1)).astype(BF16)
-    with scope('pick_half'):
-        arrived('picked', pk.at[6, lo])
-        pick_ref[...] = pk[6]
     with scope('drain'):
-        for n in range(LAYERS):
-            sent(('gather', n), panel.at[n, pl.ds(0, 7)])
-            sent(('items', n), psend.at[n])
-            sent(('sum', n), sacc.at[n, pl.ds(1, 3)])
-            sent(('zsum', n), uin.at[n])
-        for n in range(LAYERS + 1):
-            sent(('zgather', n), upan.at[n, pl.ds(0, 3)])
+        sent('gather', panel.at[:, pl.ds(0, 7)])
+        sent('items', psend)
+        sent('sum', sacc.at[:, pl.ds(1, 3)])
+        sent('zsum', uin)
+        sent('zgather', upan.at[:, pl.ds(0, 3)])
         for out, whole in (('dp', deg_send), ('zd', udeg_in), ('ds', deg_in), ('far', far_in),
-                           ('df', deg_fin), ('pick', pk.at[0]), ('picks', pick_all), ('picked', pk.at[6, lo])):
+                           ('df', deg_fin)):
             sent(out, whole)
 
 
@@ -507,7 +546,7 @@
         kernel,
         out_shape=(pltpu.VMEM((EMB, per), BF16),
                    pltpu.VMEM((EMB, width), BF16),
-                   pltpu.VMEM((EMB, n_query), BF16)),
+                   pltpu.VMEM((n_query, EMB), BF16)),
         in_specs=[hbm, hbm, hbm, hbm],
         out_specs=(vmem, vmem, vmem),
         scratch_shapes=scratch,
@@ -522,7 +561,7 @@
               pltpu.make_async_copy(user_ref, fu_ref, sem.at[1])]
     for copy in copies:
         copy.start()
-    picked = pick_ref[...].astype(F32).T.astype(BF16)
+    picked = pick_ref[...]
     cols = scores.shape[1] // 4
     for i in range(4):
         at = pl.ds(i * cols, cols)
@@ -534,12 +573,12 @@
         copy.wait()
 
 
-def outputs(fu_t, fi_t, picked_t):
-    n_query = picked_t.shape[1]
+def outputs(fu_t, fi_t, picked):
+    n_query = picked.shape[0]
     width, per = fi_t.shape[1], fu_t.shape[1]
     hbm = pl.BlockSpec(memory_space=pl.ANY)
     vmem = pl.BlockSpec(memory_space=pltpu.VMEM)
-    args = [pltpu.with_memory_space_constraint(x, pltpu.VMEM) for x in (picked_t, fi_t, fu_t)]
+    args = [pltpu.with_memory_space_constraint(x, pltpu.VMEM) for x in (picked, fi_t, fu_t)]
     return pl.pallas_call(
         output_kernel,
         out_shape=(jax.ShapeDtypeStruct((n_query, width), F32),
@@ -554,8 +593,8 @@
 
 def solution(mesh):
     def device_step(mask_blk, user_shard, item_shard, queries):
-        fu_t, fi_t, picked_t = propagate(mask_blk, user_shard.T, item_shard.T, queries)
-        scores, fi_t, fu_t = outputs(fu_t, fi_t, picked_t)
+        fu_t, fi_t, picked = propagate(mask_blk, user_shard.T, item_shard.T, queries)
+        scores, fi_t, fu_t = outputs(fu_t, fi_t, picked)
         return fu_t.T, fi_t.T, scores
 
     return jax.shard_map(

time: 94.6 us -> 94.2 us (level)
  no operation moved by 1% of the time
where the time goes in v5:
time: 94.2 us; the launch traced here: 94 us
  Pallas kernels  93.2 us (99%)
    pallas_call x1, Pallas kernels, propagate(): pl.pallas_call(kernel, out_shape=(pltpu.VMEM((EMB, per), BF16), pltpu.VME...  91.6 us

profile of v5, /device:TPU:0, one launch (start us, length us, event | category | flops | bytes accessed | tf_op | source)
XLA Modules:
  0.0 94.0 jit_solution(18082578151717551061)
XLA Ops:
  0.6 91.6 %propagate.1 = (bf16[64,128]{1,0:T(8,128)(2,1)S(1)}, bf16[64,2048]{1,0:T(8,128)(2,1)S(1)}, bf16[256,64]{1,0:T(8,128)(2,1)S(1)}) custom-call(s32[512,16384]{1,0:T(8,128)} %mask_ref.1, bf16[64,2048]{1,0:T(8,128)(2,1)} %bitcast.5, bf16[64,128]{1,0:T(8,128)(2,1)} %bitcast.6, s32[1,256]{1,0:T(1,128)} %bitcast.7), custom_call_target="tpu_custom_call" | custom-call | tf_op jit(solution)/shard_map/propagate/pallas_call | solution.py:545
  92.2 1.6 %outputs.1 = (f32[256,2048]{1,0:T(8,128)}, bf16[64,2048]{1,0:T(8,128)(2,1)}, bf16[64,128]{1,0:T(8,128)(2,1)}) custom-call(bf16[256,64]{1,0:T(8,128)(2,1)S(1)} %get-tuple-element.9.pick_ref, bf16[64,2048]{1,0:T(8,128)(2,1)S(1)} %get-tuple-element.10.item_ref, bf16[64,128]{1,0:T(8,128)(2,1)S(1)} %get-tuple-element.11.user_ref), custom_call_target="tpu_custom_call" | custom-call | tf_op jit(solution)/shard_map/outputs/pallas_call | solution.py:582

commit v6 on v5

--- a/solution.py
+++ b/solution.py
@@ -24,7 +24,7 @@
 
 
 def kernel(mask_ref, item_ref, user_ref, query_ref, fu_ref, fi_ref, pick_ref,
-           adj, stage, panel, upan, psend, drecv, sacc, hop1, rown, isum, usum,
+           adj, stage, panel, upan, psend, drecv, sacc, hop1, hop1b, rown, isum, usum,
            colacc, rowacc, deg_send, deg_recv, deg_own, deg_in, deg_fin, deg_oth, far_send, far_in,
            udeg, udeg_in, invu, uacc, upart, uin, pk, qbuf, stage_sem, in_sem, send_sem, recv_sem):
     c = lax.axis_index('col')
@@ -35,15 +35,18 @@
     per_slot = users // rows
     core, cx, cy = r % 2, (r // 2) % 2, r // 4
 
+    def flip(bit, by):
+        return (bit + by) % 2
+
     def plane(d, k):
-        return ((cy + d // 2) % 2) * 4 + ((cx + d % 2) % 2) * 2 + (core + k) % 2
+        return flip(cy, d // 2) * 4 + flip(cx, d % 2) * 2 + flip(core, k)
 
     def zpeer(k):
-        return ((c // 2 + k // 2) % 2) * 2 + (c % 2 + k % 2) % 2
+        return flip(c // 2, k // 2) * 2 + flip(c % 2, k % 2)
 
     slots = {d * 2 + k: (c, plane(d, k)) for d in range(4) for k in range(2)}
     partner, xn, yn, dg = slots[1], slots[2], slots[4], slots[6]
-    zn = [None] + [(zpeer(k), r) for k in (1, 2, 3)]
+    zn = {k: (zpeer(k), r) for k in (1, 2, 3)}
 
     got_index, out_index = {}, {}
 
@@ -92,7 +95,7 @@
         copy.start()
 
     barrier = pltpu.get_barrier_semaphore()
-    peers = tuple(slots[k] for k in range(1, 8)) + (zn[1], zn[2], zn[3])
+    peers = [device for k, device in slots.items() if k] + [zn[k] for k in (1, 2, 3)]
     for device in peers:
         pl.semaphore_signal(barrier, inc=1, device_id=device, device_id_type=pl.DeviceIdType.MESH)
 
@@ -174,8 +177,14 @@
 
         return carry
 
+    def column_sum(slot):
+        return jnp.sum(colacc[slot], axis=0, keepdims=True)
+
+    def mask_part(first, last):
+        lax.fori_loop(steps * first // 8, steps * last // 8, mask_step, 0)
+
     with jax.named_scope('mask_a'):
-        lax.fori_loop(0, steps // 4, mask_step, 0)
+        mask_part(0, 1)
     with jax.named_scope('barrier'):
         pl.semaphore_wait(barrier, len(peers))
     with jax.named_scope('inputs'):
@@ -187,19 +196,26 @@
         isum[...] = panel[0, 0].astype(F32)
         usum[...] = upan[0, c].astype(F32)
     with jax.named_scope('mask_b'):
-        lax.fori_loop(steps // 4, steps * 5 // 8, mask_step, 0)
+        mask_part(1, 5)
         for d in range(4):
-            deg_send[d:d + 1, :] = jnp.sum(colacc[2 * d + 1], axis=0, keepdims=True)
+            deg_send[pl.ds(d, 1), :] = column_sum(2 * d + 1)
         send(deg_send, deg_recv, partner, 'dp', 'dp')
+        mask_part(5, 6)
+    with jax.named_scope('forward00'):
+        gather_forward(0, 0)
     with jax.named_scope('mask_c'):
-        lax.fori_loop(steps * 5 // 8, steps, mask_step, 0)
+        mask_part(6, 7)
+    with jax.named_scope('forward01'):
+        gather_forward(0, 1)
+    with jax.named_scope('mask_d'):
+        mask_part(7, 8)
 
     with jax.named_scope('deg_sum'):
         udeg[...] = dot(jnp.ones((8, 128), BF16), rowacc[...].astype(BF16), NT)
         for k in (3, 2, 1):
             send(udeg, udeg_in.at[k - 1], zn[k], 'zd', 'zd')
         mine = jnp.concatenate(
-            [jnp.sum(colacc[2 * d], axis=0, keepdims=True) for d in range(4)], axis=0)
+            [column_sum(2 * d) for d in range(4)], axis=0)
     with jax.named_scope('deg_partner'):
         arrived('dp', deg_recv)
         deg_own[...] = mine + deg_recv[...]
@@ -210,27 +226,26 @@
             send(far_send.at[d], far_in.at[d], slots[2 * (3 - d) + 1], 'far', 'far')
     with jax.named_scope('deg_users'):
         arrived('zd', udeg_in)
-        du = (udeg[...] + udeg_in[0]) + (udeg_in[1] + udeg_in[2])
+        du = udeg[...] + jnp.sum(udeg_in[...], axis=0)
         inv = lax.rsqrt(jnp.maximum(du, 1.0))
         invu[...] = jnp.broadcast_to(inv[0:1, :], (128, users)).T
     with jax.named_scope('deg_items'):
         arrived('ds', deg_in)
     with jax.named_scope('deg_inv'):
         for d in range(4):
-            total = ((deg_own[d:d + 1, :] + deg_in[0, (d ^ 1):(d ^ 1) + 1, :])
-                     + (deg_in[1, (d ^ 2):(d ^ 2) + 1, :] + deg_in[2, (d ^ 3):(d ^ 3) + 1, :]))
-            deg_fin[d:d + 1, :] = lax.rsqrt(jnp.maximum(total, 1.0))
+            total = deg_own[pl.ds(d, 1), :]
+            for k in range(3):
+                total = total + deg_in[k, pl.ds(d ^ (k + 1), 1), :]
+            deg_fin[pl.ds(d, 1), :] = lax.rsqrt(jnp.maximum(total, 1.0))
         send(deg_fin, deg_oth, partner, 'df', 'df')
         arrived('far', far_in)
-        for i in (0, 1):
-            gather_forward(0, i)
         gather_near(0)
 
     def normalize(slot, at=0, size=width):
         d = slot // 2
         cols = pl.ds(at, size)
         if slot == 7:
-            total = (far_in[3, :, cols] + far_in[2, :, cols]) + (far_in[1, :, cols] + far_in[0, :, cols])
+            total = jnp.sum(far_in[:, :, cols], axis=0)
             inv_item = lax.rsqrt(jnp.maximum(total, 1.0))
         else:
             inv_item = (deg_oth if slot % 2 else deg_fin)[d:d + 1, cols]
@@ -274,49 +289,52 @@
         sacc[n, d] = part
 
     def items_first(u):
+        n, d = 0, 3
+
         def theirs(i):
             cols = splits[i]
-            normalize(7, starts[i], sizes[i])
-            psend[0, 3, :, cols] = dot(u, adj[7, :, cols], NN)
-            send(psend.at[0, 3, :, cols], drecv.at[0, 3, :, cols], partner, ('partner', 0, 3, i), 'items')
+            normalize(2 * d + 1, starts[i], sizes[i])
+            psend[n, d, :, cols] = dot(u, adj[2 * d + 1, :, cols], NN)
+            if i:
+                send(psend.at[n, d, :, cols], drecv.at[n, d, :, cols], partner, ('partner', n, d, i), 'items')
+            else:
+                for k, half in enumerate((lo, hi)):
+                    send(psend.at[n, d, half, cols], hop1b.at[k], slots[3 + 2 * k], 'hop1b', 'items')
 
         def ours(i):
             cols = splits[i]
-            normalize(6, starts[i], sizes[i])
-            sacc[0, 3, :, cols] = dot(u, adj[6, :, cols], NN)
+            normalize(2 * d, starts[i], sizes[i])
+            sacc[n, d, :, cols] = dot(u, adj[2 * d, :, cols], NN)
 
         def both(i):
             cols = splits[i]
-            with jax.named_scope(f'w6{i}'):
-                arrived(('partner', 0, 3, i), drecv.at[0, 3, :, cols])
-                sacc[0, 3, :, cols] = sacc[0, 3, :, cols] + drecv[0, 3, :, cols]
-            items_diagonal(0, i)
+            arrived(('partner', n, d, i), drecv.at[n, d, :, cols])
+            sacc[n, d, :, cols] = sacc[n, d, :, cols] + drecv[n, d, :, cols]
+            items_diagonal(n, i)
 
         theirs(0)
         ours(0)
+        items_diagonal(n, 0)
         theirs(1)
         theirs(2)
-        both(0)
-        ours(1)
-        both(1)
-        ours(2)
-        both(2)
+        for i in (1, 2):
+            ours(i)
+            both(i)
         arrived('df', deg_oth)
 
-        normalize(3)
-        away(0, u, 1)
-        normalize(5)
-        away(0, u, 2)
+        for k in (1, 2):
+            normalize(2 * k + 1)
+            away(n, u, k)
         normalize(2)
-        near(0, u, 1)
-        items_x(0)
+        near(n, u, 1)
+        items_x(n)
+        normalize(4)
+        near(n, u, 2)
+        items_y(n)
         normalize(1)
-        away(0, u, 0)
-        normalize(4)
-        near(0, u, 2)
-        items_y(0)
+        away(n, u, 0)
         normalize(0)
-        near(0, u, 0)
+        near(n, u, 0)
 
     def items_later(n, u, hooks):
         away(n, u, 3)
@@ -334,11 +352,15 @@
     def items_mid(n, i):
         if i == 0:
             arrived(('hop1', n), hop1.at[n])
+            if n == 0:
+                arrived('hop1b', hop1b)
+                for k in range(2):
+                    hop1[n, k, :, splits[0]] = hop1[n, k, :, splits[0]] + hop1b[k]
         at = pl.ds(i * QUARTER, QUARTER)
-        sacc[n, 2, piece(0, i)] = sacc[n, 2, piece(0, i)] + hop1[n, 0, at]
-        send(sacc.at[n, 2, piece(0, i)], rown.at[n, 2, at], yn, ('hop2', n, i), 'sum')
-        sacc[n, 1, piece(1, i)] = sacc[n, 1, piece(1, i)] + hop1[n, 1, at]
-        send(sacc.at[n, 1, piece(1, i)], rown.at[n, 1, at], xn, ('hop2', n, i), 'sum')
+        for h, device in enumerate((yn, xn)):
+            block, part = 2 - h, piece(h, i)
+            sacc[n, block, part] = sacc[n, block, part] + hop1[n, h, at]
+            send(sacc.at[n, block, part], rown.at[n, block, at], device, ('hop2', n, i), 'sum')
 
     def items_finish(n, i):
         if i == 0:
@@ -366,13 +388,13 @@
         arrived(('p0', n), panel.at[n, 1])
         uacc[...] = dot(adj[0], panel[n, 0], NT)
         some(1, 1, 1)
+        if hook is not None:
+            hook()
         if not near_done:
             gather_near(n)
         some(2, 2, 2)
         arrived(('p12', n), panel.at[n, pl.ds(2, 2)])
         some(3, 2, 2)
-        if hook is not None:
-            hook()
         gather_last(n)
         some(6, 1, 1)
         arrived(('p3', n), panel.at[n, 7])
@@ -394,10 +416,6 @@
         with scope(f'forward{n}{i}'):
             gather_forward(n, i)
 
-    def launch1():
-        forward(1, 1)
-        items_diagonal(1)
-
     def nothing():
         pass
 
@@ -406,7 +424,7 @@
     with scope('items0'):
         items_first(u0)
     with scope('user0'):
-        zsum_start(0, user_partial(0, near_done=True, hook=lambda: mid(0)))
+        zsum_start(0, user_partial(0, True, lambda: mid(0)))
     finish(0, 0)
     with scope('zsum0'):
         upan[1, c] = zsum_wait(0)
@@ -416,7 +434,7 @@
         u1 = zgather_wait(1)
     with scope('items1'):
         forward(1, 0)
-        items_later(1, u1, (nothing, launch1, nothing))
+        items_later(1, u1, (lambda: forward(1, 1), lambda: items_diagonal(1), nothing))
         items_x(1)
         items_y(1)
     with scope('user1'):
@@ -426,10 +444,11 @@
     with scope('zsum1'):
         upan[2, c] = zsum_wait(1)
         zgather_start(2)
+    finish(1, 0)
     with scope('zgather2'):
         u2 = zgather_wait(2)
     with scope('items2'):
-        items_later(2, u2, (lambda: finish(1, 0), lambda: finish(1, 1), lambda: forward(2, 0)))
+        items_later(2, u2, (nothing, lambda: finish(1, 1), lambda: forward(2, 0)))
         forward(2, 1)
         items_diagonal(2)
         items_x(2)
@@ -475,7 +494,10 @@
         @pl.when(core == 1)
         def _():
             arrived('picks', pk.at[pl.ds(3, 3)])
-            pk[6] = (pk[2] + pk[3]) + (pk[4] + pk[5])
+            total = pk[2]
+            for k in range(3):
+                total = total + pk[3 + k]
+            pk[6] = total
             send(pk.at[6], pk.at[6], partner, 'picked', 'picked')
             sent('picks', pk.at[pl.ds(3, 3)])
             sent('picked', pk.at[6])
@@ -516,6 +538,7 @@
         pltpu.VMEM((LAYERS, 4, EMB, width), F32),
         pltpu.VMEM((LAYERS, 4, EMB, width), F32),
         pltpu.VMEM((LAYERS, 2, HALF, width), F32),
+        pltpu.VMEM((2, HALF, width // 8), F32),
         pltpu.VMEM((LAYERS, 4, HALF, width), F32),
         pltpu.VMEM((EMB, width), F32),
         pltpu.VMEM((EMB, per), F32),

time: 94.2 us -> 93.7 us (level)
  no operation moved by 1% of the time
where the time goes in v6:
time: 93.7 us; the launch traced here: 93.6 us
  Pallas kernels  92.8 us (99%)
    pallas_call x1, Pallas kernels, propagate(): pl.pallas_call(kernel, out_shape=(pltpu.VMEM((EMB, per), BF16), pltpu.VME...  91.2 us

profile of v6, /device:TPU:0, one launch (start us, length us, event | category | flops | bytes accessed | tf_op | source)
XLA Modules:
  0.0 93.6 jit_solution(2310501941550049770)
XLA Ops:
  0.6 91.2 %propagate.1 = (bf16[64,128]{1,0:T(8,128)(2,1)S(1)}, bf16[64,2048]{1,0:T(8,128)(2,1)S(1)}, bf16[256,64]{1,0:T(8,128)(2,1)S(1)}) custom-call(s32[512,16384]{1,0:T(8,128)} %mask_ref.1, bf16[64,2048]{1,0:T(8,128)(2,1)} %bitcast.5, bf16[64,128]{1,0:T(8,128)(2,1)} %bitcast.6, s32[1,256]{1,0:T(1,128)} %bitcast.7), custom_call_target="tpu_custom_call" | custom-call | tf_op jit(solution)/shard_map/propagate/pallas_call | solution.py:568
  91.9 1.6 %outputs.1 = (f32[256,2048]{1,0:T(8,128)}, bf16[64,2048]{1,0:T(8,128)(2,1)}, bf16[64,128]{1,0:T(8,128)(2,1)}) custom-call(bf16[256,64]{1,0:T(8,128)(2,1)S(1)} %get-tuple-element.9.pick_ref, bf16[64,2048]{1,0:T(8,128)(2,1)S(1)} %get-tuple-element.10.item_ref, bf16[64,128]{1,0:T(8,128)(2,1)S(1)} %get-tuple-element.11.user_ref), custom_call_target="tpu_custom_call" | custom-call | tf_op jit(solution)/shard_map/outputs/pallas_call | solution.py:605

commit v7 on v6

--- a/solution.py
+++ b/solution.py
@@ -46,6 +46,8 @@
 
     slots = {d * 2 + k: (c, plane(d, k)) for d in range(4) for k in range(2)}
     partner, xn, yn, dg = slots[1], slots[2], slots[4], slots[6]
+    far_z = 3 - (c + 1) // 2 % 2
+    zorder = (far_z, 5 - far_z, 1)
     zn = {k: (zpeer(k), r) for k in (1, 2, 3)}
 
     got_index, out_index = {}, {}
@@ -131,8 +133,8 @@
         send(panel.at[n, 6], panel.at[n, 7], partner, ('p3', n), 'gather')
 
     def zgather_start(n):
-        for k in (3, 2, 1):
-            send(upan.at[n, c], upan.at[n, c], zn[k], 'zgather', 'zgather')
+        for k in zorder:
+            send(upan.at[n, c], upan.at[n, c], (zpeer(k), r), 'zgather', 'zgather')
 
     def zgather_wait(n):
         arrived('zgather', upan.at[n, pl.ds(0, 3)])
@@ -142,8 +144,8 @@
         acc_t = acc.T
         for k in range(4):
             upart[n, k] = acc_t[:, k * 128:(k + 1) * 128]
-        for k in (3, 2, 1):
-            send(upart.at[n, zpeer(k)], uin.at[n, k - 1], zn[k], 'zsum', 'zsum')
+        for k in zorder:
+            send(upart.at[n, zpeer(k)], uin.at[n, k - 1], (zpeer(k), r), 'zsum', 'zsum')
 
     def zsum_wait(n):
         arrived('zsum', uin.at[n])
@@ -212,8 +214,8 @@
 
     with jax.named_scope('deg_sum'):
         udeg[...] = dot(jnp.ones((8, 128), BF16), rowacc[...].astype(BF16), NT)
-        for k in (3, 2, 1):
-            send(udeg, udeg_in.at[k - 1], zn[k], 'zd', 'zd')
+        for k in zorder:
+            send(udeg, udeg_in.at[k - 1], (zpeer(k), r), 'zd', 'zd')
         mine = jnp.concatenate(
             [column_sum(2 * d) for d in range(4)], axis=0)
     with jax.named_scope('deg_partner'):

time: 93.7 us -> 93.8 us (level)
  no operation moved by 1% of the time
where the time goes in v7:
time: 93.8 us; the launch traced here: 93.6 us
  Pallas kernels  92.8 us (99%)
    pallas_call x1, Pallas kernels, propagate(): pl.pallas_call(kernel, out_shape=(pltpu.VMEM((EMB, per), BF16), pltpu.VME...  91.3 us

profile of v7, /device:TPU:0, one launch (start us, length us, event | category | flops | bytes accessed | tf_op | source)
XLA Modules:
  0.0 93.6 jit_solution(6954366946364873095)
XLA Ops:
  0.6 91.3 %propagate.1 = (bf16[64,128]{1,0:T(8,128)(2,1)S(1)}, bf16[64,2048]{1,0:T(8,128)(2,1)S(1)}, bf16[256,64]{1,0:T(8,128)(2,1)S(1)}) custom-call(s32[512,16384]{1,0:T(8,128)} %mask_ref.1, bf16[64,2048]{1,0:T(8,128)(2,1)} %bitcast.5, bf16[64,128]{1,0:T(8,128)(2,1)} %bitcast.6, s32[1,256]{1,0:T(1,128)} %bitcast.7), custom_call_target="tpu_custom_call" | custom-call | tf_op jit(solution)/shard_map/propagate/pallas_call | solution.py:570
  91.9 1.6 %outputs.1 = (f32[256,2048]{1,0:T(8,128)}, bf16[64,2048]{1,0:T(8,128)(2,1)}, bf16[64,128]{1,0:T(8,128)(2,1)}) custom-call(bf16[256,64]{1,0:T(8,128)(2,1)S(1)} %get-tuple-element.9.pick_ref, bf16[64,2048]{1,0:T(8,128)(2,1)S(1)} %get-tuple-element.10.item_ref, bf16[64,128]{1,0:T(8,128)(2,1)S(1)} %get-tuple-element.11.user_ref), custom_call_target="tpu_custom_call" | custom-call | tf_op jit(solution)/shard_map/outputs/pallas_call | solution.py:607

commit v8 on v7

--- a/solution.py
+++ b/solution.py
@@ -87,14 +87,14 @@
             stage.at[step % STAGES], stage_sem.at[step % STAGES])
 
     steps = 8 * per_slot
-    for s in range(STAGES):
-        mask_copy(jnp.int32(s)).start()
-
     inputs = [pltpu.make_async_copy(item_ref, panel.at[0, 0], in_sem.at[0]),
               pltpu.make_async_copy(user_ref, upan.at[0, c], in_sem.at[1]),
               pltpu.make_async_copy(query_ref, qbuf, in_sem.at[2])]
     for copy in inputs:
         copy.start()
+    for s in range(STAGES):
+        mask_copy(jnp.int32(s)).start()
+
 
     barrier = pltpu.get_barrier_semaphore()
     peers = [device for k, device in slots.items() if k] + [zn[k] for k in (1, 2, 3)]

time: 93.8 us -> 93.4 us (level)
  no operation moved by 1% of the time
where the time goes in v8:
time: 93.4 us; the launch traced here: 93.2 us
  Pallas kernels  92.4 us (99%)
    pallas_call x1, Pallas kernels, propagate(): pl.pallas_call(kernel, out_shape=(pltpu.VMEM((EMB, per), BF16), pltpu.VME...  90.8 us

profile of v8, /device:TPU:0, one launch (start us, length us, event | category | flops | bytes accessed | tf_op | source)
XLA Modules:
  0.0 93.2 jit_solution(13098556405070959603)
XLA Ops:
  0.6 90.8 %propagate.1 = (bf16[64,128]{1,0:T(8,128)(2,1)S(1)}, bf16[64,2048]{1,0:T(8,128)(2,1)S(1)}, bf16[256,64]{1,0:T(8,128)(2,1)S(1)}) custom-call(s32[512,16384]{1,0:T(8,128)} %mask_ref.1, bf16[64,2048]{1,0:T(8,128)(2,1)} %bitcast.5, bf16[64,128]{1,0:T(8,128)(2,1)} %bitcast.6, s32[1,256]{1,0:T(1,128)} %bitcast.7), custom_call_target="tpu_custom_call" | custom-call | tf_op jit(solution)/shard_map/propagate/pallas_call | solution.py:570
  91.4 1.6 %outputs.1 = (f32[256,2048]{1,0:T(8,128)}, bf16[64,2048]{1,0:T(8,128)(2,1)}, bf16[64,128]{1,0:T(8,128)(2,1)}) custom-call(bf16[256,64]{1,0:T(8,128)(2,1)S(1)} %get-tuple-element.9.pick_ref, bf16[64,2048]{1,0:T(8,128)(2,1)S(1)} %get-tuple-element.10.item_ref, bf16[64,128]{1,0:T(8,128)(2,1)S(1)} %get-tuple-element.11.user_ref), custom_call_target="tpu_custom_call" | custom-call | tf_op jit(solution)/shard_map/outputs/pallas_call | solution.py:607

commit v9 on v8

--- a/solution.py
+++ b/solution.py
@@ -202,11 +202,10 @@
         for d in range(4):
             deg_send[pl.ds(d, 1), :] = column_sum(2 * d + 1)
         send(deg_send, deg_recv, partner, 'dp', 'dp')
-        mask_part(5, 6)
     with jax.named_scope('forward00'):
         gather_forward(0, 0)
     with jax.named_scope('mask_c'):
-        mask_part(6, 7)
+        mask_part(5, 7)
     with jax.named_scope('forward01'):
         gather_forward(0, 1)
     with jax.named_scope('mask_d'):

time: 93.4 us -> 93.8 us (level)
  no operation moved by 1% of the time
where the time goes in v9:
time: 93.8 us; the launch traced here: 93.6 us
  Pallas kernels  92.8 us (99%)
    pallas_call x1, Pallas kernels, propagate(): pl.pallas_call(kernel, out_shape=(pltpu.VMEM((EMB, per), BF16), pltpu.VME...  91.3 us

profile of v9, /device:TPU:0, one launch (start us, length us, event | category | flops | bytes accessed | tf_op | source)
XLA Modules:
  0.0 93.6 jit_solution(15123567127851463544)
XLA Ops:
  0.6 91.3 %propagate.1 = (bf16[64,128]{1,0:T(8,128)(2,1)S(1)}, bf16[64,2048]{1,0:T(8,128)(2,1)S(1)}, bf16[256,64]{1,0:T(8,128)(2,1)S(1)}) custom-call(s32[512,16384]{1,0:T(8,128)} %mask_ref.1, bf16[64,2048]{1,0:T(8,128)(2,1)} %bitcast.5, bf16[64,128]{1,0:T(8,128)(2,1)} %bitcast.6, s32[1,256]{1,0:T(1,128)} %bitcast.7), custom_call_target="tpu_custom_call" | custom-call | tf_op jit(solution)/shard_map/propagate/pallas_call | solution.py:569
  91.9 1.6 %outputs.1 = (f32[256,2048]{1,0:T(8,128)}, bf16[64,2048]{1,0:T(8,128)(2,1)}, bf16[64,128]{1,0:T(8,128)(2,1)}) custom-call(bf16[256,64]{1,0:T(8,128)(2,1)S(1)} %get-tuple-element.9.pick_ref, bf16[64,2048]{1,0:T(8,128)(2,1)S(1)} %get-tuple-element.10.item_ref, bf16[64,128]{1,0:T(8,128)(2,1)S(1)} %get-tuple-element.11.user_ref), custom_call_target="tpu_custom_call" | custom-call | tf_op jit(solution)/shard_map/outputs/pallas_call | solution.py:606
